TPU v7x, 64 devices: a 2x2x8 block of a 4x4x8 slice. The times are simulated.
64 devices in a mesh: dp: 4 (over x, y), sp: 16 (over z, core).
Axes of the slice: x: 2, y: 2, z: 8, core: 2. Of those that a mesh axis runs over, the one named last changes fastest.
The devices are a block of a 4x4x8 slice.
Arguments:
- patches: bfloat16 [8, 4096, 1536], P('dp', 'sp'), parts along dimension 0
- vis_mask: int32 [8, 4096], P('dp', 'sp'), parts along dimension 0
- enc_pos: bfloat16 [16384, 1024], P(('dp', 'sp')), parts along dimension 0
- dec_pos: bfloat16 [16384, 512], P(('dp', 'sp')), parts along dimension 0
- w_pe: bfloat16 [1536, 1024], replicated
- b_pe: bfloat16 [1024], replicated
- enc_qkv: bfloat16 [2, 1024, 3, 16, 64], replicated
- enc_proj: bfloat16 [2, 16, 64, 1024], replicated
- enc_up: bfloat16 [2, 1024, 4096], replicated
- enc_down: bfloat16 [2, 4096, 1024], replicated
- w_ed: bfloat16 [1024, 512], replicated
- mask_token: bfloat16 [512], replicated
- dec_qkv: bfloat16 [2, 512, 3, 16, 32], replicated
- dec_proj: bfloat16 [2, 16, 32, 512], replicated
- dec_up: bfloat16 [2, 512, 2048], replicated
- dec_down: bfloat16 [2, 2048, 512], replicated
- w_out: bfloat16 [512, 1536], replicated
Outputs:
- output: float32 [8, 4096, 1536], P('dp', 'sp'), parts along dimension 0
There are 4 independent parts. A program takes and returns all parts, laid end to end along the dimension named above; an argument that names none is the same for every part.
All inputs are finite; a program needn't handle non-finite values.
Results may differ from a plain program's by a relative error of at most 0.0157389.
Values are sent between devices in bfloat16 or wider.
A program may use at most 768 MiB of HBM per device.

v0:
```python
import jax
import jax.numpy as jnp
from jax import lax
from jax.sharding import PartitionSpec as P

KEEP_DIV = 8


def layer_norm(hidden):
    hid_f32 = hidden.astype(jnp.float32)
    centred = hid_f32 - jnp.mean(hid_f32, axis=-1, keepdims=True)
    row_var = jnp.mean(centred * centred, axis=-1, keepdims=True)
    return (centred * lax.rsqrt(row_var + 1e-6)).astype(jnp.bfloat16)


def attn_mlp_block(hidden, w_qkv, w_proj, w_up, w_down):
    proj_qkv = jnp.einsum('cnd,dshk->scnhk', layer_norm(hidden), w_qkv, preferred_element_type=jnp.float32).astype(jnp.bfloat16)
    kv_all = lax.all_gather(proj_qkv[1:], 'sp', axis=2, tiled=True)
    scores = jnp.einsum('cqhk,cshk->chqs', proj_qkv[0], kv_all[0], preferred_element_type=jnp.float32) * proj_qkv.shape[-1] ** -0.5
    attn_probs = jax.nn.softmax(scores, axis=-1).astype(jnp.bfloat16)
    attended = jnp.einsum('chqs,cshk->cqhk', attn_probs, kv_all[1], preferred_element_type=jnp.float32).astype(jnp.bfloat16)
    mid_state = (hidden + jnp.einsum('cqhk,hkd->cqd', attended, w_proj, preferred_element_type=jnp.float32)).astype(jnp.bfloat16)
    up_act = jax.nn.gelu(jnp.einsum('cnd,df->cnf', layer_norm(mid_state), w_up, preferred_element_type=jnp.float32), approximate=False).astype(jnp.bfloat16)
    return (mid_state + jnp.einsum('cnf,fd->cnd', up_act, w_down, preferred_element_type=jnp.float32)).astype(jnp.bfloat16)


def solution(mesh):
    group_size = mesh.shape['sp']
    to_next = [(src_dev, src_dev + 1) for src_dev in range(group_size - 1)]
    to_prev = [(src_dev + 1, src_dev) for src_dev in range(group_size - 1)]

    def local_program(patches, vis_mask, enc_pos, dec_pos, w_pe, b_pe, enc_qkv, enc_proj, enc_up, enc_down, w_ed, mask_token, dec_qkv, dec_proj, dec_up, dec_down, w_out):
        vis_shard = patches.shape[1] // KEEP_DIV
        half_rows = vis_shard // 2
        my_index = lax.axis_index('sp')
        vis_counts = lax.all_gather(jnp.sum(vis_mask, axis=1), 'sp')
        vis_before = jnp.sum(jnp.where(jnp.arange(group_size)[:, None] < my_index, vis_counts, 0), axis=0)
        local_rank = jnp.cumsum(vis_mask, axis=1) - vis_mask
        dest_row = vis_before[:, None] + local_rank - my_index * vis_shard + half_rows
        row_ids = jnp.arange(2 * vis_shard)
        select = ((dest_row[:, None, :] == row_ids[None, :, None]) & (vis_mask[:, None, :] == 1)).astype(jnp.bfloat16)
        moved_x = jnp.einsum('cqi,cip->cqp', select, patches, preferred_element_type=jnp.float32).astype(jnp.bfloat16)
        moved_pos = jnp.einsum('cqi,id->cqd', select, enc_pos, preferred_element_type=jnp.float32)
        occupied = jnp.sum(select, axis=2, dtype=jnp.float32)
        embedded = (jnp.einsum('cqp,pd->cqd', moved_x, w_pe, preferred_element_type=jnp.float32)
                    + occupied[:, :, None] * b_pe.astype(jnp.float32) + moved_pos).astype(jnp.bfloat16)
        from_prev = lax.ppermute(embedded[:, 3 * half_rows:], 'sp', to_next)
        from_next = lax.ppermute(embedded[:, :half_rows], 'sp', to_prev)
        hidden = embedded[:, half_rows:3 * half_rows] + jnp.concatenate([from_prev, from_next], axis=1)
        for layer_idx in range(enc_qkv.shape[0]):
            hidden = attn_mlp_block(hidden, enc_qkv[layer_idx], enc_proj[layer_idx], enc_up[layer_idx], enc_down[layer_idx])
        z_enc = jnp.einsum('cnd,de->cne', layer_norm(hidden), w_ed, preferred_element_type=jnp.float32).astype(jnp.bfloat16)
        z_prev = lax.ppermute(z_enc[:, half_rows:], 'sp', to_next)
        z_next = lax.ppermute(z_enc[:, :half_rows], 'sp', to_prev)
        z_rows = jnp.concatenate([z_prev, z_enc, z_next], axis=1)
        placed = jnp.einsum('cqi,cqe->cie', select, z_rows, preferred_element_type=jnp.float32)
        masked_part = (1 - vis_mask).astype(jnp.float32)[:, :, None] * mask_token.astype(jnp.float32)
        hidden = (placed + masked_part + dec_pos.astype(jnp.float32)).astype(jnp.bfloat16)
        for layer_idx in range(dec_qkv.shape[0]):
            hidden = attn_mlp_block(hidden, dec_qkv[layer_idx], dec_proj[layer_idx], dec_up[layer_idx], dec_down[layer_idx])
        return jnp.einsum('cne,ep->cnp', layer_norm(hidden), w_out, preferred_element_type=jnp.float32)

    row_spec = P('dp', 'sp', None)
    pos_spec = P(('dp', 'sp'), None)
    arg_specs = (row_spec, P('dp', 'sp'), pos_spec, pos_spec) + (P(),) * 13
    return jax.shard_map(local_program, mesh=mesh, in_specs=arg_specs, out_specs=row_spec, check_vma=False)
```

profile of v0, /device:TPU:21, one launch (start us, length us, event | category | flops | bytes accessed | tf_op | source)
XLA Modules:
  0.0 640.5 jit_solution(5059401124312654784)
XLA Ops:
  11.2 16.1 %all-reduce = s32[32]{0:T(128)S(1)} all-reduce(s32[32]{0:T(128)S(1)} %dynamic-update-slice), channel_id=2, replica_groups=mesh['dp'=4,'sp'=16] {'sp'}, use_global_device_ids=true, to_apply=%add | all-reduce | flops 32 | bytes 256
  34.6 5.4 collective-permute-start
  42.0 3.6 collective-permute-done.1
  46.0 5.9 fusion.114
  53.1 49.6 %all-gather.6.cloned.1.call-done = bf16[2,2,512,16,64]{4,2,3,0,1:T(8,128)(2,1)} async-done(((bf16[2,2,32,16,64]{4,2,3,0,1:T(8,128)(2,1)}), bf16[2,2,512,16,64]{4,2,3,0,1:T(8,128)(2,1)}) %all-gather.6.cloned.1.call-update) | async-done | bytes 4194320 | tf_op jit(solution)/shard_map/all_gather | solution.py:18
  102.7 3.7 fusion.47
  107.0 5.1 fusion.529
  112.4 5.4 fusion.345
  117.8 6.1 fusion.532
  124.2 3.1 fusion.111
  128.6 50.8 %all-gather.8.cloned.1.call-done = bf16[2,2,512,16,64]{4,2,3,0,1:T(8,128)(2,1)} async-done(((bf16[2,2,32,16,64]{4,2,3,0,1:T(8,128)(2,1)}), bf16[2,2,512,16,64]{4,2,3,0,1:T(8,128)(2,1)}) %all-gather.8.cloned.1.call-update) | async-done | bytes 4194320 | tf_op jit(solution)/shard_map/all_gather | solution.py:18
  179.4 3.7 fusion.45
  183.7 5.1 fusion.534
  189.0 5.3 fusion.346
  194.3 6.0 fusion.537
  205.6 2.7 collective-permute-done.3
  212.0 97.5 %all-gather.10.cloned.1.call-done = bf16[2,2,4096,16,32]{2,4,3,0,1:T(8,128)(2,1)} async-done(((bf16[2,2,256,16,32]{2,4,3,0,1:T(8,128)(2,1)}), bf16[2,2,4096,16,32]{2,4,3,0,1:T(8,128)(2,1)}) %all-gather.10.cloned.1.call-update) | async-done | bytes 16777232 | tf_op jit(solution)/shard_map/all_gather | solution.py:18
  309.5 51.3 %fusion.538 = (f32[2,16,256]{2,1,0:T(8,128)S(1)}, f32[2,16,256,4096]{3,2,1,0:T(8,128)}) fusion(bf16[2,2,4096,16,32]{2,4,3,0,1:T(8,128)(2,1)} %all-gather.10.cloned.1.call-done, bf16[3,2,256,16,32]{2,4,3,0,1:T(8,128)(2,1)S(1)} %fusion.90), kind=kOutput, calls=%fused_computation.566 | convolution fusion | flops 2248151040 | bytes 143163392 | tf_op jit(solution)/shard_map/sub | solution.py:20
  360.7 45.6 %fusion.148 = bf16[2,256,16,32]{1,3,2,0:T(8,128)(2,1)S(1)} fusion(f32[2,16,256,4096]{3,2,1,0:T(8,128)} %get-tuple-element.34, f32[2,16,256]{2,1,0:T(8,128)S(1)} %get-tuple-element.33, bf16[2,2,4096,16,32]{2,4,3,0,1:T(8,128)(2,1)} %all-gather.10.cloned.1.call-done), kind=kOutput, calls=%fused_computation.175 | convolution fusion | flops 2214854656 | bytes 143163392 | tf_op jit(solution)/shard_map/chqs,cshk->cqhk/dot_general | solution.py:21
  410.9 10.0 %convert_reduce_fusion.1 = (f32[2,256]{1,0:T(2,128)S(1)}, bf16[2,256,512]{2,1,0:T(8,128)(2,1)S(1)}) fusion(bf16[2,2048,512]{2,1,0:T(8,128)(2,1)S(1)} %copy-done.12, f32[2,256,2048]{2,1,0:T(8,128)S(1)} %get-tuple-element.37, u8[256,2048]{1,0:T(8,128)(4,1)S(1)} %get-tuple-element.8, u8[256,2048]{1,0:T(8,128)(4,1)S(1)} %get-tuple-element.7, ...), kind=kOutput, calls=%fused_computation.134 | convolution fusion | flops 1148452352 | bytes 8390656 | tf_op jit(solution)/shard_map/cnf,fd->cnd/dot_general | solution.py:24
  423.5 95.8 %all-gather.12.cloned.1.call-done = bf16[2,2,4096,16,32]{2,4,3,0,1:T(8,128)(2,1)} async-done(((bf16[2,2,256,16,32]{2,4,3,0,1:T(8,128)(2,1)}), bf16[2,2,4096,16,32]{2,4,3,0,1:T(8,128)(2,1)}) %all-gather.12.cloned.1.call-update) | async-done | bytes 16777232 | tf_op jit(solution)/shard_map/all_gather | solution.py:18
  519.3 51.3 %fusion.539 = (f32[2,16,256]{2,1,0:T(8,128)S(1)}, f32[2,16,256,4096]{3,2,1,0:T(8,128)}) fusion(bf16[2,2,4096,16,32]{2,4,3,0,1:T(8,128)(2,1)} %all-gather.12.cloned.1.call-done, bf16[3,2,256,16,32]{2,4,3,0,1:T(8,128)(2,1)S(1)} %fusion.93), kind=kOutput, calls=%fused_computation.567 | convolution fusion | flops 2248151040 | bytes 143163392 | tf_op jit(solution)/shard_map/sub | solution.py:20
  570.5 45.8 %fusion.149 = bf16[2,256,16,32]{1,3,2,0:T(8,128)(2,1)S(1)} fusion(f32[2,16,256,4096]{3,2,1,0:T(8,128)} %get-tuple-element.41, f32[2,16,256]{2,1,0:T(8,128)S(1)} %get-tuple-element.40, bf16[2,2,4096,16,32]{2,4,3,0,1:T(8,128)(2,1)} %all-gather.12.cloned.1.call-done), kind=kOutput, calls=%fused_computation.176 | convolution fusion | flops 2214854656 | bytes 143163392 | tf_op jit(solution)/shard_map/chqs,cshk->cqhk/dot_general | solution.py:21
  620.9 9.8 %convert_reduce_fusion.4 = (f32[2,256]{1,0:T(2,128)S(1)}, bf16[2,256,512]{2,1,0:T(8,128)(2,1)S(1)}) fusion(bf16[2,2048,512]{2,1,0:T(8,128)(2,1)S(1)} %copy-done.13, f32[2,256,2048]{2,1,0:T(8,128)S(1)} %get-tuple-element.44, u8[256,2048]{1,0:T(8,128)(4,1)S(1)} %get-tuple-element.6, u8[256,2048]{1,0:T(8,128)(4,1)S(1)} %get-tuple-element.5, ...), kind=kOutput, calls=%fused_computation.153 | convolution fusion | flops 1148452352 | bytes 8390656 | tf_op jit(solution)/shard_map/cnf,fd->cnd/dot_general | solution.py:24
  (124 shorter events, 41.2 us)
Async XLA Ops:
  6.5 25.6 %copy-start = (bf16[1536,1024]{1,0:T(8,128)(2,1)S(1)}, bf16[1536,1024]{1,0:T(8,128)(2,1)}, u32[]{:S(2)}) copy-start(bf16[1536,1024]{1,0:T(8,128)(2,1)} %param.21) | copy-start | bytes 9437188
  6.6 96.2 %all-gather.6.cloned.1.call-start = ((), (), s32[]{:S(2)}) async-start(), calls=%async_computation | async-start | bytes 8912896 | tf_op jit(solution)/shard_map/all_gather | solution.py:18
  34.6 7.4 %collective-permute-start = (bf16[2,16,1024]{2,1,0:T(8,128)(2,1)S(1)}, bf16[2,16,1024]{2,1,0:T(8,128)(2,1)S(1)}, u32[]{:S(2)}, u32[]{:S(2)}) collective-permute-start(bf16[2,16,1024]{2,1,0:T(8,128)(2,1)S(1)} %get-tuple-element.15), channel_id=1, source_target_pairs={{0,1},{1,2},{2,3},{3,4},{4,5},{5,6},{6,7},{7,8},{8,9},{9,10},{10,1... | collective-permute-start | bytes 196616 | tf_op jit(solution)/shard_map/ppermute | solution.py:47
  40.0 5.6 collective-permute-start.1
  52.8 126.6 %all-gather.8.cloned.1.call-start = ((), (), s32[]{:S(2)}) async-start(), calls=%async_computation.1 | async-start | bytes 8912896 | tf_op jit(solution)/shard_map/all_gather | solution.py:18
  112.4 11.8 %slice-start = ((s8[12582912]{0:T(1024)(128)(4,1)}), s8[4194304]{0:T(1024)(128)(4,1)S(1)}, s32[]{:S(2)}) async-start(s8[12582912]{0:T(1024)(128)(4,1)} %bitcast.341), calls=%async_computation.4 | async-start | bytes 8388608
  117.8 6.3 slice-start.1
  117.8 6.3 slice-start.2
  128.2 181.3 %all-gather.10.cloned.1.call-start = ((), (), s32[]{:S(2)}) async-start(), calls=%async_computation.2 | async-start | bytes 17825792 | tf_op jit(solution)/shard_map/all_gather | solution.py:18
  194.3 6.3 copy-start.3
  194.3 11.2 %copy-start.9 = (bf16[512]{0:T(512)(128)(2,1)S(1)}, bf16[512]{0:T(512)(128)(2,1)}, u32[]{:S(2)}) copy-start(bf16[512]{0:T(512)(128)(2,1)} %param.28) | copy-start | bytes 3076
  194.3 11.2 %copy-start.8 = (bf16[256,512]{1,0:T(8,128)(2,1)S(1)}, bf16[256,512]{1,0:T(8,128)(2,1)}, u32[]{:S(2)}) copy-start(bf16[256,512]{1,0:T(8,128)(2,1)} %param.20) | copy-start | bytes 786436
  200.4 8.7 %copy-start.14 = (bf16[2,512,3,16,32]{1,4,3,2,0:T(8,128)(2,1)S(1)}, bf16[2,512,3,16,32]{1,4,3,2,0:T(8,128)(2,1)}, u32[]{:S(2)}) copy-start(bf16[2,512,3,16,32]{1,4,3,2,0:T(8,128)(2,1)} %param.29) | copy-start | bytes 9437188
  201.0 4.6 collective-permute-start.2
  203.1 5.3 collective-permute-start.3
  211.4 307.9 %all-gather.12.cloned.1.call-start = ((), (), s32[]{:S(2)}) async-start(), calls=%async_computation.3 | async-start | bytes 17825792 | tf_op jit(solution)/shard_map/all_gather | solution.py:18
  360.7 45.6 %copy-start.5 = (bf16[2,256,512]{2,1,0:T(8,128)(2,1)S(1)}, bf16[2,256,512]{2,1,0:T(8,128)(2,1)}, u32[]{:S(2)}) copy-start(bf16[2,256,512]{2,1,0:T(8,128)(2,1)} %copy-done.4) | copy-start | bytes 1572868
  360.7 45.6 %copy-start.16 = (bf16[2,16,32,512]{3,2,1,0:T(8,128)(2,1)S(1)}, bf16[2,16,32,512]{3,2,1,0:T(8,128)(2,1)}, u32[]{:S(2)}) copy-start(bf16[2,16,32,512]{3,2,1,0:T(8,128)(2,1)} %param.30) | copy-start | bytes 3145732
  410.9 10.4 %copy-start.15 = (bf16[2,512,3,16,32]{1,4,3,2,0:T(8,128)(2,1)S(1)}, bf16[2,512,3,16,32]{1,4,3,2,0:T(8,128)(2,1)}, u32[]{:S(2)}) copy-start(bf16[2,512,3,16,32]{1,4,3,2,0:T(8,128)(2,1)} %param.29) | copy-start | bytes 9437188
  420.9 2.6 copy-start.6
  570.5 45.8 %copy-start.7 = (bf16[2,256,512]{2,1,0:T(8,128)(2,1)S(1)}, bf16[2,256,512]{2,1,0:T(8,128)(2,1)}, u32[]{:S(2)}) copy-start(bf16[2,256,512]{2,1,0:T(8,128)(2,1)} %copy-done.6) | copy-start | bytes 1572868
  570.5 45.8 %copy-start.17 = (bf16[2,16,32,512]{3,2,1,0:T(8,128)(2,1)S(1)}, bf16[2,16,32,512]{3,2,1,0:T(8,128)(2,1)}, u32[]{:S(2)}) copy-start(bf16[2,16,32,512]{3,2,1,0:T(8,128)(2,1)} %param.30) | copy-start | bytes 3145732
  620.9 10.2 %copy-start.2 = (bf16[512,1536]{1,0:T(8,128)(2,1)S(1)}, bf16[512,1536]{1,0:T(8,128)(2,1)}, u32[]{:S(2)}) copy-start(bf16[512,1536]{1,0:T(8,128)(2,1)} %param.33) | copy-start | bytes 4718596
  620.9 12.9 %copy-start.1 = (bf16[1536,1024]{1,0:T(8,128)(2,1)S(1)}, bf16[1536,1024]{1,0:T(8,128)(2,1)}, u32[]{:S(2)}) copy-start(bf16[1536,1024]{1,0:T(8,128)(2,1)} %param.21) | copy-start | bytes 9437188
  (5 other events, 11.6 us)
Sparse Core Ops, SparseCore 0:
  52.9 49.7 all-gather.5
  128.3 51.0 all-gather.7
  211.5 97.9 all-gather.9
  423.6 95.6 all-gather.11
where the time goes:
time: 645 us; the launch traced here: 640 us
  waiting for transfers between devices  300 us (47%)
  matrix products  279 us (43%)
  blocking collectives  16.1 us (2%)
  between operations  14.4 us (2%)
  starting transfers between devices  13.2 us (2%)
  local copies, waits for them, and re-layouts  9.06 us (1%)
  other arithmetic  8.18 us (1%)
    all_gather x4, waiting for transfers between devices, attn_mlp_block(): kv_all = lax.all_gather(proj_qkv[1:], 'sp', axis=2, tiled=True)  294 us
    sub x2, matrix products, attn_mlp_block(): attn_probs = jax.nn.softmax(scores, axis=-1).astype(jnp.bfloat16)  103 us
    dot_general x2, matrix products, attn_mlp_block(): jnp.einsum('chqs,cshk->cqhk', attn_probs, kv_all[1], preferred_element_ty...  91.4 us
    dot_general x4, matrix products, attn_mlp_block(): jnp.einsum('cnf,fd->cnd', up_act, w_down, preferred_element_type=jnp.floa...  32 us
    unnamed x1, blocking collectives  16.1 us
    dot_general x4, matrix products, attn_mlp_block(): jnp.einsum('cnd,df->cnf', layer_norm(mid_state), w_up, preferred_element_...  15.3 us
  transfers between devices with their start and end apart: 8, of which 6 were waited for; matrix products, arithmetic and copies ran while one was open for 0% of the time, Pallas kernels for 0%

commit v1 on v0

--- a/solution.py
+++ b/solution.py
@@ -1,9 +1,18 @@
+import functools
+
 import jax
 import jax.numpy as jnp
 from jax import lax
+from jax.experimental import pallas as pl
+from jax.experimental.pallas import tpu as pltpu
 from jax.sharding import PartitionSpec as P
 
 KEEP_DIV = 8
+PIECES = 2
+MESH = pl.DeviceIdType.MESH
+LOG2E = 1.4426950408889634
+NT = (((1,), (1,)), ((), ()))
+TN = (((0,), (0,)), ((), ()))
 
 
 def layer_norm(hidden):
@@ -11,6 +20,14 @@
     centred = hid_f32 - jnp.mean(hid_f32, axis=-1, keepdims=True)
     row_var = jnp.mean(centred * centred, axis=-1, keepdims=True)
     return (centred * lax.rsqrt(row_var + 1e-6)).astype(jnp.bfloat16)
+
+
+def gelu(x):
+    return 0.5 * x * (1.0 + lax.erf(x * 0.7071067811865476))
+
+
+def fdot(lhs, rhs, dims=(((1,), (0,)), ((), ()))):
+    return lax.dot_general(lhs, rhs, dims, preferred_element_type=jnp.float32)
 
 
 def attn_mlp_block(hidden, w_qkv, w_proj, w_up, w_down):
@@ -22,6 +39,214 @@
     mid_state = (hidden + jnp.einsum('cqhk,hkd->cqd', attended, w_proj, preferred_element_type=jnp.float32)).astype(jnp.bfloat16)
     up_act = jax.nn.gelu(jnp.einsum('cnd,df->cnf', layer_norm(mid_state), w_up, preferred_element_type=jnp.float32), approximate=False).astype(jnp.bfloat16)
     return (mid_state + jnp.einsum('cnf,fd->cnd', up_act, w_down, preferred_element_type=jnp.float32)).astype(jnp.bfloat16)
+
+
+class RingGather:
+    def __init__(self, n_chips, piece_rows, buf, send, recv):
+        self.n, self.rows, self.buf, self.send, self.recv = n_chips, piece_rows, buf, send, recv
+        me = lax.axis_index('sp')
+        size = 2 * n_chips
+        self.right = lax.rem(me + 2, size)
+        self.left = lax.rem(me + size - 2, size)
+        self.mate = me + 1 - 2 * lax.rem(me, 2)
+        self.arrivals = PIECES * (n_chips // 2) - 1
+
+    def barrier(self):
+        sem = pltpu.get_barrier_semaphore()
+        for peer in (self.left, self.right, self.mate):
+            pl.semaphore_signal(sem, inc=1, device_id={'sp': peer}, device_id_type=MESH)
+        pl.semaphore_wait(sem, 3)
+
+    def copy(self, phase, kind, step, piece):
+        if kind == 2:
+            src, dst, dst_core, peer = step, step, 1, self.mate
+        elif kind == 0:
+            src, dst, dst_core, peer = step, step + 1, 0, self.right
+        else:
+            src, dst, dst_core, peer = lax.rem(self.n - step, self.n), self.n - 1 - step, 0, self.left
+        rows = pl.ds(pl.multiple_of(piece * self.rows, self.rows), self.rows)
+        return pltpu.make_async_remote_copy(
+            src_ref=self.buf.at[phase, src, 0, rows], dst_ref=self.buf.at[phase, dst, dst_core, rows],
+            send_sem=self.send.at[phase, kind, step, piece], recv_sem=self.recv.at[phase, kind, step, piece],
+            device_id={'sp': peer}, device_id_type=MESH)
+
+    def begin(self, phase):
+        for piece in range(PIECES):
+            self.copy(phase, 0, 0, piece).start()
+            self.copy(phase, 1, 0, PIECES - 1 - piece).start()
+            self.copy(phase, 2, 0, piece).start()
+
+    def relay(self, phase, k):
+        step = k // PIECES
+        p_right = lax.rem(k, PIECES)
+        p_left = PIECES - 1 - p_right
+        self.copy(phase, 0, step, p_right).wait_recv()
+        pl.when(k < self.arrivals - PIECES)(lambda: self.copy(phase, 0, step + 1, p_right).start())
+        self.copy(phase, 2, step + 1, p_right).start()
+        self.copy(phase, 1, step, p_left).wait_recv()
+        pl.when(k < self.arrivals - PIECES)(lambda: self.copy(phase, 1, step + 1, p_left).start())
+        self.copy(phase, 2, self.n - 1 - step, p_left).start()
+
+    def finish(self, phase):
+        def per_slot(i, carry):
+            mate_copy = self.copy(phase, 2, i // PIECES, lax.rem(i, PIECES))
+            mate_copy.wait_recv()
+            mate_copy.wait_send()
+            return carry
+
+        def per_hop(k, carry):
+            self.copy(phase, 0, k // PIECES, lax.rem(k, PIECES)).wait_send()
+            self.copy(phase, 1, k // PIECES, PIECES - 1 - lax.rem(k, PIECES)).wait_send()
+            return carry
+
+        lax.fori_loop(0, PIECES * self.n, per_slot, 0)
+        lax.fori_loop(0, self.arrivals, per_hop, 0)
+
+
+def decoder_kernel(n_chips, n_heads, u_ref, wqkv_hbm, wproj_hbm, wup_hbm, wdown_hbm, state,
+                   gath, k_ref, vt_ref, s_ref, m_ref, qm_ref, ot_ref, wqkv, wproj, wup, wdown, send, recv, wsem):
+    n_clips, rows, width = u_ref.shape
+    n_layers = wproj.shape[0]
+    phases = n_layers * n_clips
+    head_dim = width // n_heads
+    lane_heads = qm_ref.shape[1] // head_dim
+    chunk = 2 * rows
+    scale = head_dim ** -0.5 * LOG2E
+    ring = RingGather(n_chips, rows // PIECES, gath, send, recv)
+
+    weights = [pltpu.make_async_copy(src, dst, wsem.at[i]) for i, (src, dst) in enumerate(
+        ((wqkv_hbm, wqkv), (wproj_hbm, wproj), (wup_hbm, wup), (wdown_hbm, wdown)))]
+    for copy in weights:
+        copy.start()
+    for clip in range(n_clips):
+        state[clip] = u_ref[clip]
+        gath[clip, 0, 0] = layer_norm(u_ref[clip])
+    qm_ref[...] = jnp.zeros_like(qm_ref)
+    ring.barrier()
+    ring.begin(0)
+    lax.fori_loop(0, ring.arrivals, lambda k, carry: (ring.relay(0, k), carry)[1], 0)
+    for copy in weights:
+        copy.wait()
+
+    def scores(head, j, slot, top):
+        group = head // lane_heads
+        keys = k_ref[j, :, pl.ds(pl.multiple_of(group * qm_ref.shape[1], qm_ref.shape[1]), qm_ref.shape[1])]
+        s = fdot(keys, qm_ref[head]).reshape(chunk // 8, 8, rows)
+        s_ref[slot, j] = s
+        return jnp.maximum(top, jnp.max(s, axis=0))
+
+    def set_top(slot, top):
+        m_ref[slot] = jnp.broadcast_to(jnp.max(top, axis=0, keepdims=True), top.shape)
+
+    def values(head, j, slot, total, acc):
+        e = jnp.exp2((s_ref[slot, j] - m_ref[slot][None]) * scale)
+        vt = vt_ref[j, pl.ds(pl.multiple_of(head * head_dim, head_dim), head_dim), :]
+        return total + jnp.sum(e, axis=0), acc + fdot(vt, e.reshape(chunk, rows).astype(jnp.bfloat16))
+
+    def put_out(head, total, acc):
+        out = acc * (1.0 / jnp.sum(total, axis=0, keepdims=True))
+        ot_ref[pl.ds(pl.multiple_of(head * head_dim, head_dim), head_dim), :] = out.astype(jnp.bfloat16)
+
+    low = jnp.full((8, rows), -jnp.inf, jnp.float32)
+    none = jnp.zeros((8, rows), jnp.float32)
+    zero = jnp.zeros((head_dim, rows), jnp.float32)
+
+    def phase_body(phase, carry):
+        clip = lax.rem(phase, n_clips)
+        layer = phase // n_clips
+        more = phase + 1 < phases
+        ring.finish(phase)
+        pl.when(more)(lambda: ring.begin(phase + 1))
+
+        def project(r, carry):
+            a = gath[phase, r].reshape(chunk, width)
+            k_ref[r] = fdot(a, wqkv[layer, 1], NT).astype(jnp.bfloat16)
+            vt_ref[r] = fdot(wqkv[layer, 2], a, NT).astype(jnp.bfloat16)
+            return carry
+
+        lax.fori_loop(0, n_chips, project, 0)
+        qt = fdot(wqkv[layer, 0], gath[phase, 0, 0], NT).astype(jnp.bfloat16)
+        for head in range(n_heads):
+            at = (head % lane_heads) * head_dim
+            qm_ref[head, at:at + head_dim, :] = qt[head * head_dim:(head + 1) * head_dim]
+
+        top = low
+        for j in range(n_chips):
+            top = scores(0, j, 0, top)
+        set_top(0, top)
+
+        def head_body(head, carry):
+            now = lax.rem(head, 2)
+            turn = head - 2
+            pl.when(more & (turn >= 0) & (lax.rem(turn, 2) == 0) & (turn // 2 < ring.arrivals))(
+                lambda: ring.relay(phase + 1, turn // 2))
+            top, total, acc = low, none, zero
+            for j in range(n_chips):
+                top = scores(head + 1, j, 1 - now, top)
+                total, acc = values(head, j, now, total, acc)
+            set_top(1 - now, top)
+            put_out(head, total, acc)
+            return carry
+
+        lax.fori_loop(0, n_heads - 1, head_body, 0)
+        total, acc = none, zero
+        for j in range(n_chips):
+            total, acc = values(n_heads - 1, j, (n_heads - 1) % 2, total, acc)
+        put_out(n_heads - 1, total, acc)
+
+        mid = (state[clip].astype(jnp.float32) + fdot(ot_ref[...], wproj[layer], TN)).astype(jnp.bfloat16)
+        normed = layer_norm(mid)
+        down = mid.astype(jnp.float32)
+        for f in range(0, wup.shape[2], width):
+            act = gelu(fdot(normed, wup[layer, :, f:f + width])).astype(jnp.bfloat16)
+            down = down + fdot(act, wdown[layer, f:f + width, :])
+        new = down.astype(jnp.bfloat16)
+        state[clip] = new
+
+        @pl.when(phase + n_clips < phases)
+        def _():
+            gath[phase + n_clips, 0, 0] = layer_norm(new)
+
+        return carry
+
+    lax.fori_loop(0, phases, phase_body, 0)
+
+
+def run_decoder(n_chips, u, w_qkv, w_proj, w_up, w_down):
+    n_clips, rows, width = u.shape
+    n_layers, _, _, n_heads, head_dim = w_qkv.shape
+    phases = n_layers * n_clips
+    w_qkv = jnp.transpose(w_qkv, (0, 2, 3, 4, 1)).reshape(n_layers, 3, width, width)
+    w_proj = w_proj.reshape(n_layers, width, width)
+    mlp = w_up.shape[2]
+    bf = jnp.bfloat16
+    vmem, hbm = pl.BlockSpec(memory_space=pltpu.VMEM), pl.BlockSpec(memory_space=pl.ANY)
+    keys = 2 * n_chips * rows
+    return pl.pallas_call(
+        functools.partial(decoder_kernel, n_chips, n_heads),
+        out_shape=jax.ShapeDtypeStruct(u.shape, bf),
+        in_specs=[vmem, hbm, hbm, hbm, hbm],
+        out_specs=vmem,
+        scratch_shapes=[
+            pltpu.VMEM((phases, n_chips, 2, rows, width), bf),
+            pltpu.VMEM((n_chips, 2 * rows, width), bf),
+            pltpu.VMEM((n_chips, width, 2 * rows), bf),
+            pltpu.VMEM((2, n_chips, rows // 4, 8, rows), jnp.float32),
+            pltpu.VMEM((2, 8, rows), jnp.float32),
+            pltpu.VMEM((n_heads, 256, rows), bf),
+            pltpu.VMEM((width, rows), bf),
+            pltpu.VMEM((n_layers, 3, width, width), bf),
+            pltpu.VMEM((n_layers, width, width), bf),
+            pltpu.VMEM((n_layers, width, mlp), bf),
+            pltpu.VMEM((n_layers, mlp, width), bf),
+            pltpu.SemaphoreType.DMA((phases, 3, n_chips, PIECES)),
+            pltpu.SemaphoreType.DMA((phases, 3, n_chips, PIECES)),
+            pltpu.SemaphoreType.DMA((4,)),
+        ],
+        compiler_params=pltpu.CompilerParams(collective_id=1, has_side_effects=True, vmem_limit_bytes=60 * 1024 * 1024),
+        cost_estimate=pl.CostEstimate(flops=phases * n_heads * keys * rows * 2 * (256 + head_dim), bytes_accessed=16 * 1024 * 1024, transcendentals=phases * n_heads * keys * rows),
+        name='decoder',
+    )(u, w_qkv, w_proj, w_up, w_down)
 
 
 def solution(mesh):
@@ -56,8 +281,7 @@
         placed = jnp.einsum('cqi,cqe->cie', select, z_rows, preferred_element_type=jnp.float32)
         masked_part = (1 - vis_mask).astype(jnp.float32)[:, :, None] * mask_token.astype(jnp.float32)
         hidden = (placed + masked_part + dec_pos.astype(jnp.float32)).astype(jnp.bfloat16)
-        for layer_idx in range(dec_qkv.shape[0]):
-            hidden = attn_mlp_block(hidden, dec_qkv[layer_idx], dec_proj[layer_idx], dec_up[layer_idx], dec_down[layer_idx])
+        hidden = run_decoder(group_size // 2, hidden, dec_qkv, dec_proj, dec_up, dec_down)
         return jnp.einsum('cne,ep->cnp', layer_norm(hidden), w_out, preferred_element_type=jnp.float32)
 
     row_spec = P('dp', 'sp', None)

time: 645 us -> 464 us (0.72)
  Pallas kernels: 0 us -> 240 us
  matrix products: 279 us -> 59.9 us
  waiting for transfers between devices: 300 us -> 108 us
    pallas_call x0 -> x1, Pallas kernels: none -> 240 us  [run_decoder(): pl.pallas_call(functools.partial(decoder_kernel, n_chips, n_heads), out_s...]
    all_gather x4 -> x2, waiting for transfers between devices: 294 us -> 101 us  [attn_mlp_block(): kv_all = lax.all_gather(proj_qkv[1:], 'sp', axis=2, tiled=True)]
    sub x2 -> x0, matrix products: 103 us -> none  [attn_mlp_block(): attn_probs = jax.nn.softmax(scores, axis=-1).astype(jnp.bfloat16)]
    dot_general x2 -> x0, matrix products: 91.4 us -> none  [attn_mlp_block(): jnp.einsum('chqs,cshk->cqhk', attn_probs, kv_all[1], preferred_element_ty...]
    dot_general x4 -> x2, matrix products: 32 us -> 12.3 us  [attn_mlp_block(): jnp.einsum('cnf,fd->cnd', up_act, w_down, preferred_element_type=jnp.floa...]
    dot_general x4 -> x2, matrix products: 15.3 us -> 10.7 us  [attn_mlp_block(): jnp.einsum('cnd,df->cnf', layer_norm(mid_state), w_up, preferred_element_...]
  transfers between devices with their start and end apart: 8 -> 6, of which waited for: 6 -> 4; matrix products, arithmetic and copies ran while one was open for 0% -> 0% of each run, Pallas kernels for 0% -> 0%
where the time goes in v1:
time: 464 us
  Pallas kernels  240 us (52%)
  waiting for transfers between devices  108 us (23%)
  matrix products  59.9 us (13%)
  blocking collectives  16.1 us (3%)
  between operations  14.4 us (3%)
  starting transfers between devices  11.9 us (3%)
  other arithmetic  9.08 us (2%)
    pallas_call x1, Pallas kernels, run_decoder(): pl.pallas_call(functools.partial(decoder_kernel, n_chips, n_heads), out_s...  240 us
    all_gather x2, waiting for transfers between devices, attn_mlp_block(): kv_all = lax.all_gather(proj_qkv[1:], 'sp', axis=2, tiled=True)  101 us
    unnamed x1, blocking collectives  16.1 us
    dot_general x2, matrix products, attn_mlp_block(): jnp.einsum('cnf,fd->cnd', up_act, w_down, preferred_element_type=jnp.floa...  12.3 us
    dot_general x2, matrix products, attn_mlp_block(): jnp.einsum('cnd,df->cnf', layer_norm(mid_state), w_up, preferred_element_...  10.7 us
    dot_general x2, matrix products, attn_mlp_block(): jnp.einsum('cqhk,hkd->cqd', attended, w_proj, preferred_element_type=jnp....  10.3 us
  transfers between devices with their start and end apart: 6, of which 4 were waited for; matrix products, arithmetic and copies ran while one was open for 0% of the time, Pallas kernels for 0%

profile of v1, /device:TPU:21, one launch (start us, length us, event | category | flops | bytes accessed | tf_op | source)
XLA Modules:
  0.0 463.7 jit_solution(1529508810868890322)
XLA Ops:
  11.1 16.1 %all-reduce = s32[32]{0:T(128)S(1)} all-reduce(s32[32]{0:T(128)S(1)} %dynamic-update-slice), channel_id=2, replica_groups=mesh['dp'=4,'sp'=16] {'sp'}, use_global_device_ids=true, to_apply=%add | all-reduce | flops 32 | bytes 256
  29.4 2.1 fusion.137
  32.2 2.4 fusion.58
  34.6 5.4 %collective-permute-start = (bf16[2,16,1024]{2,1,0:T(8,128)(2,1)S(1)}, bf16[2,16,1024]{2,1,0:T(8,128)(2,1)S(1)}, u32[]{:S(2)}, u32[]{:S(2)}) collective-permute-start(bf16[2,16,1024]{2,1,0:T(8,128)(2,1)S(1)} %get-tuple-element.11), channel_id=1, source_target_pairs={{0,1},{1,2},{2,3},{3,4},{4,5},{5,6},{6,7},{7,8},{8,9},{9,10},{10,1... | collective-permute-start | bytes 196616 | tf_op jit(solution)/shard_map/ppermute | solution.py:272
  40.0 2.0 collective-permute-start.1
  42.0 3.6 collective-permute-done.1
  46.0 5.9 %fusion.46 = bf16[3,2,32,16,64]{4,2,3,0,1:T(8,128)(2,1)S(1)} fusion(bf16[2,1024,3,16,64]{1,4,3,2,0:T(8,128)(2,1)} %param.23, bf16[2,32,1024]{2,1,0:T(8,128)(2,1)S(1)} %get-tuple-element.10, f32[2,32]{1,0:T(2,128)S(1)} %add_rsqrt_fusion.5, f32[2,32]{1,0:T(2,128)S(1)} %broadcast_multiply_fusion.5), kind=kOutput, calls=%fused_computation.56 | convolution fusion | flops 403111936 | bytes 6816256 | tf_op jit(solution)/shard_map/cnd,dshk->scnhk/dot_general | solution.py:34
  52.9 49.9 %all-gather.4.cloned.1.call-done = bf16[2,2,512,16,64]{4,2,3,0,1:T(8,128)(2,1)} async-done(((bf16[2,2,32,16,64]{4,2,3,0,1:T(8,128)(2,1)}), bf16[2,2,512,16,64]{4,2,3,0,1:T(8,128)(2,1)}) %all-gather.4.cloned.1.call-update) | async-done | bytes 4194320 | tf_op jit(solution)/shard_map/all_gather | solution.py:35
  102.7 3.7 fusion.23
  107.0 5.1 %fusion.339 = (f32[2,32]{1,0:T(2,128)S(1)}, f32[2,32,1024]{2,1,0:T(8,128)S(1)}) fusion(bf16[2,16,64,1024]{3,2,1,0:T(8,128)(2,1)} %param.24, bf16[2,2,512,16,64]{4,2,3,0,1:T(8,128)(2,1)} %all-gather.4.cloned.1.call-done, f32[2,16,32]{2,1,0:T(8,128)S(1)} %fusion.338, f32[2,16,32,512]{3,2,1,0:T(8,128)S(1)} %fusion.23, ...), kind=kOutput, calls=%fused_computation.342 | convolution fusion | flops 203818432 | bytes 8786176 | tf_op jit(solution)/shard_map/cqhk,hkd->cqd/dot_general | solution.py:39
  112.4 5.4 %fusion.219 = (u8[32,4096]{1,0:T(8,128)(4,1)S(1)}, u8[32,4096]{1,0:T(8,128)(4,1)S(1)}, f32[2,32,4096]{2,1,0:T(8,128)S(1)}) fusion(bf16[2,1024,4096]{2,1,0:T(8,128)(2,1)} %param.25, f32[2,32,1024]{2,1,0:T(8,128)S(1)} %get-tuple-element.18, f32[2,32]{1,0:T(2,128)S(1)} %add_rsqrt_fusion.4, f32[2,32]{1,0:T(2,128)S(1)} %broadcast_multiply_fusion.4), kind=kOutput, calls=%fused_computation.214 | convolution fusion | flops 540213248 | bytes 9961984 | tf_op jit(solution)/shard_map/cnd,df->cnf/dot_general | solution.py:40
  117.8 6.3 %fusion.342 = (f32[2,32]{1,0:T(2,128)S(1)}, f32[2,32,1024]{2,1,0:T(8,128)S(1)}) fusion(f32[2,32,1024]{2,1,0:T(8,128)S(1)} %get-tuple-element.18, bf16[2,4096,1024]{2,1,0:T(8,128)(2,1)} %param.26, f32[2,32,4096]{2,1,0:T(8,128)S(1)} %get-tuple-element.19, u8[32,4096]{1,0:T(8,128)(4,1)S(1)} %get-tuple-element.8, u8[32,4096]{1,0:T(8,128)(4,1)S(1)} %get-tuple-element.7), kind=kOutput, calls=%fused_computation.343 | convolution fusion | flops 555483072 | bytes 10223872 | tf_op jit(solution)/shard_map/cnf,fd->cnd/dot_general | solution.py:41
  124.3 3.1 fusion.43
  128.4 51.2 %all-gather.6.cloned.1.call-done = bf16[2,2,512,16,64]{4,2,3,0,1:T(8,128)(2,1)} async-done(((bf16[2,2,32,16,64]{4,2,3,0,1:T(8,128)(2,1)}), bf16[2,2,512,16,64]{4,2,3,0,1:T(8,128)(2,1)}) %all-gather.6.cloned.1.call-update) | async-done | bytes 4194320 | tf_op jit(solution)/shard_map/all_gather | solution.py:35
  179.6 3.7 fusion.21
  183.9 5.1 %fusion.344 = (f32[2,32]{1,0:T(2,128)S(1)}, f32[2,32,1024]{2,1,0:T(8,128)S(1)}) fusion(f32[2,32,1024]{2,1,0:T(8,128)S(1)} %get-tuple-element.21, bf16[2,16,64,1024]{3,2,1,0:T(8,128)(2,1)} %param.24, bf16[2,2,512,16,64]{4,2,3,0,1:T(8,128)(2,1)} %all-gather.6.cloned.1.call-done, f32[2,16,32]{2,1,0:T(8,128)S(1)} %fusion.343, f32[2,16,32,512]{3,2,1,0:T(8,128)S(1)} %fusion.21), kind=kOutput, calls=%fused_computation.345 | convolution fusion | flops 203752896 | bytes 8917248 | tf_op jit(solution)/shard_map/cqhk,hkd->cqd/dot_general | solution.py:39
  189.2 5.3 %fusion.220 = (u8[32,4096]{1,0:T(8,128)(4,1)S(1)}, u8[32,4096]{1,0:T(8,128)(4,1)S(1)}, f32[2,32,4096]{2,1,0:T(8,128)S(1)}) fusion(bf16[2,1024,4096]{2,1,0:T(8,128)(2,1)} %param.25, f32[2,32,1024]{2,1,0:T(8,128)S(1)} %get-tuple-element.23, f32[2,32]{1,0:T(2,128)S(1)} %add_rsqrt_fusion.2, f32[2,32]{1,0:T(2,128)S(1)} %broadcast_multiply_fusion.2), kind=kOutput, calls=%fused_computation.215 | convolution fusion | flops 540213248 | bytes 9961984 | tf_op jit(solution)/shard_map/cnd,df->cnf/dot_general | solution.py:40
  194.5 6.0 %fusion.347 = (f32[2,32]{1,0:T(2,128)S(1)}, f32[2,32,1024]{2,1,0:T(8,128)S(1)}) fusion(f32[2,32,1024]{2,1,0:T(8,128)S(1)} %get-tuple-element.23, bf16[2,4096,1024]{2,1,0:T(8,128)(2,1)} %param.26, f32[2,32,4096]{2,1,0:T(8,128)S(1)} %get-tuple-element.24, u8[32,4096]{1,0:T(8,128)(4,1)S(1)} %get-tuple-element.6, u8[32,4096]{1,0:T(8,128)(4,1)S(1)} %get-tuple-element.5), kind=kOutput, calls=%fused_computation.346 | convolution fusion | flops 555483072 | bytes 10223872 | tf_op jit(solution)/shard_map/cnf,fd->cnd/dot_general | solution.py:41
  201.1 2.0 collective-permute-start.2
  203.1 2.4 collective-permute-start.3
  205.6 2.7 collective-permute-done.3
  209.5 240.5 %decoder.1 = bf16[2,256,512]{2,1,0:T(8,128)(2,1)} custom-call(bf16[2,256,512]{2,1,0:T(8,128)(2,1)} %fusion.49.u_ref, bf16[2,3,512,512]{3,2,1,0:T(8,128)(2,1)} %bitcast.196, bf16[2,512,512]{2,1,0:T(8,128)(2,1)} %bitcast.197, bf16[2,512,2048]{2,1,0:T(8,128)(2,1)} %wup_hbm.1, bf16[2,2048,512]{2,1,0:T(8,128)(2,1)} %wdown_hbm.1), custom_call_target="tpu_custom_call" | custom-call | flops 38654705664 | bytes 16777216 | tf_op jit(solution)/shard_map/decoder/pallas_call | solution.py:225
  451.2 1.3 fusion.107
  452.5 4.3 fusion.34
  (68 shorter events, 13.8 us)
Async XLA Ops:
  6.5 25.6 %copy-start = (bf16[1536,1024]{1,0:T(8,128)(2,1)S(1)}, bf16[1536,1024]{1,0:T(8,128)(2,1)}, u32[]{:S(2)}) copy-start(bf16[1536,1024]{1,0:T(8,128)(2,1)} %param.21) | copy-start | bytes 9437188
  6.6 96.2 %all-gather.4.cloned.1.call-start = ((), (), s32[]{:S(2)}) async-start(), calls=%async_computation | async-start | bytes 8912896 | tf_op jit(solution)/shard_map/all_gather | solution.py:35
  34.6 7.4 %collective-permute-start = (bf16[2,16,1024]{2,1,0:T(8,128)(2,1)S(1)}, bf16[2,16,1024]{2,1,0:T(8,128)(2,1)S(1)}, u32[]{:S(2)}, u32[]{:S(2)}) collective-permute-start(bf16[2,16,1024]{2,1,0:T(8,128)(2,1)S(1)} %get-tuple-element.11), channel_id=1, source_target_pairs={{0,1},{1,2},{2,3},{3,4},{4,5},{5,6},{6,7},{7,8},{8,9},{9,10},{10,1... | collective-permute-start | bytes 196616 | tf_op jit(solution)/shard_map/ppermute | solution.py:272
  40.0 5.6 %collective-permute-start.1 = (bf16[2,16,1024]{2,1,0:T(8,128)(2,1)S(1)}, bf16[2,16,1024]{2,1,0:T(8,128)(2,1)S(1)}, u32[]{:S(2)}, u32[]{:S(2)}) collective-permute-start(bf16[2,16,1024]{2,1,0:T(8,128)(2,1)S(1)} %get-tuple-element.12), channel_id=1, source_target_pairs={{1,0},{2,1},{3,2},{4,3},{5,4},{6,5},{7,6},{8,7},{9,8},{10,9},{11,1... | collective-permute-start | bytes 196616 | tf_op jit(solution)/shard_map/ppermute | solution.py:273
  52.8 126.8 %all-gather.6.cloned.1.call-start = ((), (), s32[]{:S(2)}) async-start(), calls=%async_computation.1 | async-start | bytes 8912896 | tf_op jit(solution)/shard_map/all_gather | solution.py:35
  112.4 11.9 %slice-start = ((s8[12582912]{0:T(1024)(128)(4,1)}), s8[4194304]{0:T(1024)(128)(4,1)S(1)}, s32[]{:S(2)}) async-start(s8[12582912]{0:T(1024)(128)(4,1)} %bitcast.194), calls=%async_computation.2 | async-start | bytes 8388608
  117.8 6.5 %slice-start.1 = ((s8[12582912]{0:T(1024)(128)(4,1)}), s8[4194304]{0:T(1024)(128)(4,1)S(1)}, s32[]{:S(2)}) async-start(s8[12582912]{0:T(1024)(128)(4,1)} %bitcast.194), calls=%async_computation.3 | async-start | bytes 8388608
  117.8 6.5 %slice-start.2 = ((s8[12582912]{0:T(1024)(128)(4,1)}), s8[4194304]{0:T(1024)(128)(4,1)S(1)}, s32[]{:S(2)}) async-start(s8[12582912]{0:T(1024)(128)(4,1)} %bitcast.194), calls=%async_computation.4 | async-start | bytes 8388608
  194.5 6.3 %copy-start.2 = (bf16[1024,512]{1,0:T(8,128)(2,1)S(1)}, bf16[1024,512]{1,0:T(8,128)(2,1)}, u32[]{:S(2)}) copy-start(bf16[1024,512]{1,0:T(8,128)(2,1)} %param.27) | copy-start | bytes 3145732
  194.5 11.1 %copy-start.3 = (bf16[256,512]{1,0:T(8,128)(2,1)S(1)}, bf16[256,512]{1,0:T(8,128)(2,1)}, u32[]{:S(2)}) copy-start(bf16[256,512]{1,0:T(8,128)(2,1)} %param.20) | copy-start | bytes 786436
  194.5 11.1 %copy-start.4 = (bf16[512]{0:T(512)(128)(2,1)S(1)}, bf16[512]{0:T(512)(128)(2,1)}, u32[]{:S(2)}) copy-start(bf16[512]{0:T(512)(128)(2,1)} %param.28) | copy-start | bytes 3076
  201.1 4.5 collective-permute-start.2
  203.1 5.3 %collective-permute-start.3 = (bf16[2,16,512]{2,1,0:T(8,128)(2,1)S(1)}, bf16[2,16,512]{2,1,0:T(8,128)(2,1)S(1)}, u32[]{:S(2)}, u32[]{:S(2)}) collective-permute-start(bf16[2,16,512]{2,1,0:T(8,128)(2,1)S(1)} %get-tuple-element.14), channel_id=1, source_target_pairs={{1,0},{2,1},{3,2},{4,3},{5,4},{6,5},{7,6},{8,7},{9,8},{10,9},{11,1... | collective-permute-start | bytes 98312 | tf_op jit(solution)/shard_map/ppermute | solution.py:279
  209.5 247.3 %copy-start.1 = (bf16[1536,1024]{1,0:T(8,128)(2,1)S(1)}, bf16[1536,1024]{1,0:T(8,128)(2,1)}, u32[]{:S(2)}) copy-start(bf16[1536,1024]{1,0:T(8,128)(2,1)} %param.21) | copy-start | bytes 9437188
Sparse Core Ops, SparseCore 0:
  52.9 49.7 all-gather.3
  128.5 51.0 all-gather.5

commit v2 on v1

--- a/solution.py
+++ b/solution.py
@@ -87,24 +87,28 @@
         pl.when(k < self.arrivals - PIECES)(lambda: self.copy(phase, 1, step + 1, p_left).start())
         self.copy(phase, 2, self.n - 1 - step, p_left).start()
 
-    def finish(self, phase):
+    def take(self, phase, slot):
+        for piece in range(PIECES):
+            self.copy(phase, 2, slot, piece).wait_recv()
+
+    def drain(self, phases):
         def per_slot(i, carry):
-            mate_copy = self.copy(phase, 2, i // PIECES, lax.rem(i, PIECES))
-            mate_copy.wait_recv()
-            mate_copy.wait_send()
+            slot = lax.rem(i // PIECES, self.n)
+            self.copy(i // (PIECES * self.n), 2, slot, lax.rem(i, PIECES)).wait_send()
             return carry
 
-        def per_hop(k, carry):
+        def per_hop(i, carry):
+            phase, k = i // self.arrivals, lax.rem(i, self.arrivals)
             self.copy(phase, 0, k // PIECES, lax.rem(k, PIECES)).wait_send()
             self.copy(phase, 1, k // PIECES, PIECES - 1 - lax.rem(k, PIECES)).wait_send()
             return carry
 
-        lax.fori_loop(0, PIECES * self.n, per_slot, 0)
-        lax.fori_loop(0, self.arrivals, per_hop, 0)
+        lax.fori_loop(0, phases * PIECES * self.n, per_slot, 0)
+        lax.fori_loop(0, phases * self.arrivals, per_hop, 0)
 
 
 def decoder_kernel(n_chips, n_heads, u_ref, wqkv_hbm, wproj_hbm, wup_hbm, wdown_hbm, state,
-                   gath, k_ref, vt_ref, s_ref, m_ref, qm_ref, ot_ref, wqkv, wproj, wup, wdown, send, recv, wsem):
+                   gath, k_ref, vt_ref, s_even, s_odd, m_ref, qm_ref, ot_ref, wqkv, wproj, wup, wdown, send, recv, wsem):
     n_clips, rows, width = u_ref.shape
     n_layers = wproj.shape[0]
     phases = n_layers * n_clips
@@ -112,6 +116,7 @@
     lane_heads = qm_ref.shape[1] // head_dim
     chunk = 2 * rows
     scale = head_dim ** -0.5 * LOG2E
+    s_both = (s_even, s_odd)
     ring = RingGather(n_chips, rows // PIECES, gath, send, recv)
 
     weights = [pltpu.make_async_copy(src, dst, wsem.at[i]) for i, (src, dst) in enumerate(
@@ -124,7 +129,6 @@
     qm_ref[...] = jnp.zeros_like(qm_ref)
     ring.barrier()
     ring.begin(0)
-    lax.fori_loop(0, ring.arrivals, lambda k, carry: (ring.relay(0, k), carry)[1], 0)
     for copy in weights:
         copy.wait()
 
@@ -132,14 +136,14 @@
         group = head // lane_heads
         keys = k_ref[j, :, pl.ds(pl.multiple_of(group * qm_ref.shape[1], qm_ref.shape[1]), qm_ref.shape[1])]
         s = fdot(keys, qm_ref[head]).reshape(chunk // 8, 8, rows)
-        s_ref[slot, j] = s
+        s_both[slot][j] = s
         return jnp.maximum(top, jnp.max(s, axis=0))
 
     def set_top(slot, top):
         m_ref[slot] = jnp.broadcast_to(jnp.max(top, axis=0, keepdims=True), top.shape)
 
     def values(head, j, slot, total, acc):
-        e = jnp.exp2((s_ref[slot, j] - m_ref[slot][None]) * scale)
+        e = jnp.exp2((s_both[slot][j] - m_ref[slot][None]) * scale)
         vt = vt_ref[j, pl.ds(pl.multiple_of(head * head_dim, head_dim), head_dim), :]
         return total + jnp.sum(e, axis=0), acc + fdot(vt, e.reshape(chunk, rows).astype(jnp.bfloat16))
 
@@ -155,10 +159,16 @@
         clip = lax.rem(phase, n_clips)
         layer = phase // n_clips
         more = phase + 1 < phases
-        ring.finish(phase)
-        pl.when(more)(lambda: ring.begin(phase + 1))
-
-        def project(r, carry):
+        first = phase == 0
+        pl.when(more & (phase > 0))(lambda: ring.begin(phase + 1))
+
+        def project(i, carry):
+            odd = lax.rem(i, 2)
+            r = jnp.where(odd == 1, (i + 1) // 2, lax.rem(n_chips - i // 2, n_chips))
+            pl.when(first & (odd == 1))(lambda: ring.relay(phase, i - 1))
+            pl.when(first & (odd == 1) & (i < ring.arrivals))(lambda: ring.relay(phase, i))
+            pl.when(more & first & (i == ring.arrivals - 1))(lambda: ring.begin(phase + 1))
+            ring.take(phase, r)
             a = gath[phase, r].reshape(chunk, width)
             k_ref[r] = fdot(a, wqkv[layer, 1], NT).astype(jnp.bfloat16)
             vt_ref[r] = fdot(wqkv[layer, 2], a, NT).astype(jnp.bfloat16)
@@ -175,24 +185,27 @@
             top = scores(0, j, 0, top)
         set_top(0, top)
 
-        def head_body(head, carry):
-            now = lax.rem(head, 2)
-            turn = head - 2
-            pl.when(more & (turn >= 0) & (lax.rem(turn, 2) == 0) & (turn // 2 < ring.arrivals))(
-                lambda: ring.relay(phase + 1, turn // 2))
+        def head_step(head, now, last=False):
             top, total, acc = low, none, zero
             for j in range(n_chips):
-                top = scores(head + 1, j, 1 - now, top)
+                if not last:
+                    top = scores(head + 1, j, 1 - now, top)
                 total, acc = values(head, j, now, total, acc)
-            set_top(1 - now, top)
+            if not last:
+                set_top(1 - now, top)
             put_out(head, total, acc)
+
+        def head_pair(pair, carry):
+            late = (pair > 2).astype(jnp.int32) + (pair > 5).astype(jnp.int32)
+            pl.when(more & (pair != 2) & (pair != 5))(lambda: ring.relay(phase + 1, pair - late))
+            head_step(2 * pair, 0)
+            head_step(2 * pair + 1, 1)
             return carry
 
-        lax.fori_loop(0, n_heads - 1, head_body, 0)
-        total, acc = none, zero
-        for j in range(n_chips):
-            total, acc = values(n_heads - 1, j, (n_heads - 1) % 2, total, acc)
-        put_out(n_heads - 1, total, acc)
+        lax.fori_loop(0, n_heads // 2 - 1, head_pair, 0)
+        pl.when(more)(lambda: ring.relay(phase + 1, ring.arrivals - 2))
+        head_step(n_heads - 2, 0)
+        head_step(n_heads - 1, 1, last=True)
 
         mid = (state[clip].astype(jnp.float32) + fdot(ot_ref[...], wproj[layer], TN)).astype(jnp.bfloat16)
         normed = layer_norm(mid)
@@ -207,9 +220,11 @@
         def _():
             gath[phase + n_clips, 0, 0] = layer_norm(new)
 
+        pl.when(more)(lambda: ring.relay(phase + 1, ring.arrivals - 1))
         return carry
 
     lax.fori_loop(0, phases, phase_body, 0)
+    ring.drain(phases)
 
 
 def run_decoder(n_chips, u, w_qkv, w_proj, w_up, w_down):
@@ -231,7 +246,8 @@
             pltpu.VMEM((phases, n_chips, 2, rows, width), bf),
             pltpu.VMEM((n_chips, 2 * rows, width), bf),
             pltpu.VMEM((n_chips, width, 2 * rows), bf),
-            pltpu.VMEM((2, n_chips, rows // 4, 8, rows), jnp.float32),
+            pltpu.VMEM((n_chips, rows // 4, 8, rows), jnp.float32),
+            pltpu.VMEM((n_chips, rows // 4, 8, rows), jnp.float32),
             pltpu.VMEM((2, 8, rows), jnp.float32),
             pltpu.VMEM((n_heads, 256, rows), bf),
             pltpu.VMEM((width, rows), bf),

time: 464 us -> 360 us (0.78)
  Pallas kernels: 240 us -> 137 us
    pallas_call x1, Pallas kernels: 240 us -> 137 us  [run_decoder(): pl.pallas_call(functools.partial(decoder_kernel, n_chips, n_heads), out_s...]
where the time goes in v2:
time: 360 us
  Pallas kernels  137 us (38%)
  waiting for transfers between devices  108 us (30%)
  matrix products  59.9 us (17%)
  blocking collectives  16.1 us (4%)
  between operations  14.4 us (4%)
  starting transfers between devices  11.9 us (3%)
  other arithmetic  9.08 us (3%)
  local copies, waits for them, and re-layouts  4.37 us (1%)
    pallas_call x1, Pallas kernels, run_decoder(): pl.pallas_call(functools.partial(decoder_kernel, n_chips, n_heads), out_s...  137 us
    all_gather x2, waiting for transfers between devices, attn_mlp_block(): kv_all = lax.all_gather(proj_qkv[1:], 'sp', axis=2, tiled=True)  101 us
    unnamed x1, blocking collectives  16.1 us
    dot_general x2, matrix products, attn_mlp_block(): jnp.einsum('cnf,fd->cnd', up_act, w_down, preferred_element_type=jnp.floa...  12.3 us
    dot_general x2, matrix products, attn_mlp_block(): jnp.einsum('cnd,df->cnf', layer_norm(mid_state), w_up, preferred_element_...  10.7 us
    dot_general x2, matrix products, attn_mlp_block(): jnp.einsum('cqhk,hkd->cqd', attended, w_proj, preferred_element_type=jnp....  10.3 us
    dot_general x2, matrix products, attn_mlp_block(): jnp.einsum('cnd,dshk->scnhk', layer_norm(hidden), w_qkv, preferred_elemen...  9.07 us
    dot_general x2, matrix products, attn_mlp_block(): jnp.einsum('cqhk,cshk->chqs', proj_qkv[0], kv_all[0], preferred_element_t...  7.31 us
  transfers between devices with their start and end apart: 6, of which 4 were waited for; matrix products, arithmetic and copies ran while one was open for 0% of the time, Pallas kernels for 0%

profile of v2, /device:TPU:21, one launch (start us, length us, event | category | flops | bytes accessed | tf_op | source)
XLA Modules:
  0.0 359.8 jit_solution(2706222599019387183)
XLA Ops:
  11.1 16.1 %all-reduce = s32[32]{0:T(128)S(1)} all-reduce(s32[32]{0:T(128)S(1)} %dynamic-update-slice), channel_id=2, replica_groups=mesh['dp'=4,'sp'=16] {'sp'}, use_global_device_ids=true, to_apply=%add | all-reduce | flops 32 | bytes 256
  29.4 2.1 fusion.137
  32.2 2.4 fusion.58
  34.6 5.4 %collective-permute-start = (bf16[2,16,1024]{2,1,0:T(8,128)(2,1)S(1)}, bf16[2,16,1024]{2,1,0:T(8,128)(2,1)S(1)}, u32[]{:S(2)}, u32[]{:S(2)}) collective-permute-start(bf16[2,16,1024]{2,1,0:T(8,128)(2,1)S(1)} %get-tuple-element.11), channel_id=1, source_target_pairs={{0,1},{1,2},{2,3},{3,4},{4,5},{5,6},{6,7},{7,8},{8,9},{9,10},{10,1... | collective-permute-start | bytes 196616 | tf_op jit(solution)/shard_map/ppermute | solution.py:288
  40.0 2.0 collective-permute-start.1
  42.0 3.6 %collective-permute-done.1 = bf16[2,16,1024]{2,1,0:T(8,128)(2,1)S(1)} collective-permute-done((bf16[2,16,1024]{2,1,0:T(8,128)(2,1)S(1)}, bf16[2,16,1024]{2,1,0:T(8,128)(2,1)S(1)}, u32[]{:S(2)}, u32[]{:S(2)}) %collective-permute-start.1) | collective-permute-done | bytes 65568 | tf_op jit(solution)/shard_map/ppermute | solution.py:289
  46.0 5.9 %fusion.46 = bf16[3,2,32,16,64]{4,2,3,0,1:T(8,128)(2,1)S(1)} fusion(bf16[2,1024,3,16,64]{1,4,3,2,0:T(8,128)(2,1)} %param.23, bf16[2,32,1024]{2,1,0:T(8,128)(2,1)S(1)} %get-tuple-element.10, f32[2,32]{1,0:T(2,128)S(1)} %add_rsqrt_fusion.5, f32[2,32]{1,0:T(2,128)S(1)} %broadcast_multiply_fusion.5), kind=kOutput, calls=%fused_computation.56 | convolution fusion | flops 403111936 | bytes 6816256 | tf_op jit(solution)/shard_map/cnd,dshk->scnhk/dot_general | solution.py:34
  52.9 49.9 %all-gather.4.cloned.1.call-done = bf16[2,2,512,16,64]{4,2,3,0,1:T(8,128)(2,1)} async-done(((bf16[2,2,32,16,64]{4,2,3,0,1:T(8,128)(2,1)}), bf16[2,2,512,16,64]{4,2,3,0,1:T(8,128)(2,1)}) %all-gather.4.cloned.1.call-update) | async-done | bytes 4194320 | tf_op jit(solution)/shard_map/all_gather | solution.py:35
  102.7 3.7 %fusion.23 = f32[2,16,32,512]{3,2,1,0:T(8,128)S(1)} fusion(bf16[2,2,512,16,64]{4,2,3,0,1:T(8,128)(2,1)} %all-gather.4.cloned.1.call-done, bf16[3,2,32,16,64]{4,2,3,0,1:T(8,128)(2,1)S(1)} %fusion.46), kind=kOutput, calls=%fused_computation.27 | convolution fusion | flops 67108864 | bytes 6553600 | tf_op jit(solution)/shard_map/cqhk,cshk->chqs/dot_general | solution.py:36
  107.0 5.1 %fusion.339 = (f32[2,32]{1,0:T(2,128)S(1)}, f32[2,32,1024]{2,1,0:T(8,128)S(1)}) fusion(bf16[2,16,64,1024]{3,2,1,0:T(8,128)(2,1)} %param.24, bf16[2,2,512,16,64]{4,2,3,0,1:T(8,128)(2,1)} %all-gather.4.cloned.1.call-done, f32[2,16,32]{2,1,0:T(8,128)S(1)} %fusion.338, f32[2,16,32,512]{3,2,1,0:T(8,128)S(1)} %fusion.23, ...), kind=kOutput, calls=%fused_computation.342 | convolution fusion | flops 203818432 | bytes 8786176 | tf_op jit(solution)/shard_map/cqhk,hkd->cqd/dot_general | solution.py:39
  112.4 5.4 %fusion.219 = (u8[32,4096]{1,0:T(8,128)(4,1)S(1)}, u8[32,4096]{1,0:T(8,128)(4,1)S(1)}, f32[2,32,4096]{2,1,0:T(8,128)S(1)}) fusion(bf16[2,1024,4096]{2,1,0:T(8,128)(2,1)} %param.25, f32[2,32,1024]{2,1,0:T(8,128)S(1)} %get-tuple-element.18, f32[2,32]{1,0:T(2,128)S(1)} %add_rsqrt_fusion.4, f32[2,32]{1,0:T(2,128)S(1)} %broadcast_multiply_fusion.4), kind=kOutput, calls=%fused_computation.214 | convolution fusion | flops 540213248 | bytes 9961984 | tf_op jit(solution)/shard_map/cnd,df->cnf/dot_general | solution.py:40
  117.8 6.3 %fusion.342 = (f32[2,32]{1,0:T(2,128)S(1)}, f32[2,32,1024]{2,1,0:T(8,128)S(1)}) fusion(f32[2,32,1024]{2,1,0:T(8,128)S(1)} %get-tuple-element.18, bf16[2,4096,1024]{2,1,0:T(8,128)(2,1)} %param.26, f32[2,32,4096]{2,1,0:T(8,128)S(1)} %get-tuple-element.19, u8[32,4096]{1,0:T(8,128)(4,1)S(1)} %get-tuple-element.8, u8[32,4096]{1,0:T(8,128)(4,1)S(1)} %get-tuple-element.7), kind=kOutput, calls=%fused_computation.343 | convolution fusion | flops 555483072 | bytes 10223872 | tf_op jit(solution)/shard_map/cnf,fd->cnd/dot_general | solution.py:41
  124.3 3.1 fusion.43
  128.4 51.2 %all-gather.6.cloned.1.call-done = bf16[2,2,512,16,64]{4,2,3,0,1:T(8,128)(2,1)} async-done(((bf16[2,2,32,16,64]{4,2,3,0,1:T(8,128)(2,1)}), bf16[2,2,512,16,64]{4,2,3,0,1:T(8,128)(2,1)}) %all-gather.6.cloned.1.call-update) | async-done | bytes 4194320 | tf_op jit(solution)/shard_map/all_gather | solution.py:35
  179.6 3.7 %fusion.21 = f32[2,16,32,512]{3,2,1,0:T(8,128)S(1)} fusion(bf16[2,2,512,16,64]{4,2,3,0,1:T(8,128)(2,1)} %all-gather.6.cloned.1.call-done, bf16[3,2,32,16,64]{4,2,3,0,1:T(8,128)(2,1)S(1)} %fusion.43), kind=kOutput, calls=%fused_computation.23 | convolution fusion | flops 67108864 | bytes 6553600 | tf_op jit(solution)/shard_map/cqhk,cshk->chqs/dot_general | solution.py:36
  183.9 5.1 %fusion.344 = (f32[2,32]{1,0:T(2,128)S(1)}, f32[2,32,1024]{2,1,0:T(8,128)S(1)}) fusion(f32[2,32,1024]{2,1,0:T(8,128)S(1)} %get-tuple-element.21, bf16[2,16,64,1024]{3,2,1,0:T(8,128)(2,1)} %param.24, bf16[2,2,512,16,64]{4,2,3,0,1:T(8,128)(2,1)} %all-gather.6.cloned.1.call-done, f32[2,16,32]{2,1,0:T(8,128)S(1)} %fusion.343, f32[2,16,32,512]{3,2,1,0:T(8,128)S(1)} %fusion.21), kind=kOutput, calls=%fused_computation.345 | convolution fusion | flops 203752896 | bytes 8917248 | tf_op jit(solution)/shard_map/cqhk,hkd->cqd/dot_general | solution.py:39
  189.2 5.3 %fusion.220 = (u8[32,4096]{1,0:T(8,128)(4,1)S(1)}, u8[32,4096]{1,0:T(8,128)(4,1)S(1)}, f32[2,32,4096]{2,1,0:T(8,128)S(1)}) fusion(bf16[2,1024,4096]{2,1,0:T(8,128)(2,1)} %param.25, f32[2,32,1024]{2,1,0:T(8,128)S(1)} %get-tuple-element.23, f32[2,32]{1,0:T(2,128)S(1)} %add_rsqrt_fusion.2, f32[2,32]{1,0:T(2,128)S(1)} %broadcast_multiply_fusion.2), kind=kOutput, calls=%fused_computation.215 | convolution fusion | flops 540213248 | bytes 9961984 | tf_op jit(solution)/shard_map/cnd,df->cnf/dot_general | solution.py:40
  194.5 6.0 %fusion.347 = (f32[2,32]{1,0:T(2,128)S(1)}, f32[2,32,1024]{2,1,0:T(8,128)S(1)}) fusion(f32[2,32,1024]{2,1,0:T(8,128)S(1)} %get-tuple-element.23, bf16[2,4096,1024]{2,1,0:T(8,128)(2,1)} %param.26, f32[2,32,4096]{2,1,0:T(8,128)S(1)} %get-tuple-element.24, u8[32,4096]{1,0:T(8,128)(4,1)S(1)} %get-tuple-element.6, u8[32,4096]{1,0:T(8,128)(4,1)S(1)} %get-tuple-element.5), kind=kOutput, calls=%fused_computation.346 | convolution fusion | flops 555483072 | bytes 10223872 | tf_op jit(solution)/shard_map/cnf,fd->cnd/dot_general | solution.py:41
  201.1 2.0 collective-permute-start.2
  203.1 2.4 collective-permute-start.3
  205.6 2.7 collective-permute-done.3
  209.5 136.6 %decoder.1 = bf16[2,256,512]{2,1,0:T(8,128)(2,1)} custom-call(bf16[2,256,512]{2,1,0:T(8,128)(2,1)} %fusion.49.u_ref, bf16[2,3,512,512]{3,2,1,0:T(8,128)(2,1)} %bitcast.196, bf16[2,512,512]{2,1,0:T(8,128)(2,1)} %bitcast.197, bf16[2,512,2048]{2,1,0:T(8,128)(2,1)} %wup_hbm.1, bf16[2,2048,512]{2,1,0:T(8,128)(2,1)} %wdown_hbm.1), custom_call_target="tpu_custom_call" | custom-call | flops 38654705664 | bytes 16777216 | tf_op jit(solution)/shard_map/decoder/pallas_call | solution.py:240
  347.3 1.3 fusion.107
  348.7 4.3 %fusion.34 = f32[2,256,1536]{2,1,0:T(8,128)} fusion(bf16[512,1536]{1,0:T(8,128)(2,1)} %param.33, bf16[2,256,512]{2,1,0:T(8,128)(2,1)} %decoder.1, f32[2,256]{1,0:T(2,128)S(1)} %add_rsqrt_fusion, f32[2,256]{1,0:T(2,128)S(1)} %broadcast_multiply_fusion), kind=kOutput, calls=%fused_computation.45 | convolution fusion | flops 806354944 | bytes 5246976 | tf_op jit(solution)/shard_map/cne,ep->cnp/dot_general | solution.py:301
  (68 shorter events, 13.8 us)
Async XLA Ops:
  6.5 25.6 %copy-start = (bf16[1536,1024]{1,0:T(8,128)(2,1)S(1)}, bf16[1536,1024]{1,0:T(8,128)(2,1)}, u32[]{:S(2)}) copy-start(bf16[1536,1024]{1,0:T(8,128)(2,1)} %param.21) | copy-start | bytes 9437188
  6.6 96.2 %all-gather.4.cloned.1.call-start = ((), (), s32[]{:S(2)}) async-start(), calls=%async_computation | async-start | bytes 8912896 | tf_op jit(solution)/shard_map/all_gather | solution.py:35
  34.6 7.4 %collective-permute-start = (bf16[2,16,1024]{2,1,0:T(8,128)(2,1)S(1)}, bf16[2,16,1024]{2,1,0:T(8,128)(2,1)S(1)}, u32[]{:S(2)}, u32[]{:S(2)}) collective-permute-start(bf16[2,16,1024]{2,1,0:T(8,128)(2,1)S(1)} %get-tuple-element.11), channel_id=1, source_target_pairs={{0,1},{1,2},{2,3},{3,4},{4,5},{5,6},{6,7},{7,8},{8,9},{9,10},{10,1... | collective-permute-start | bytes 196616 | tf_op jit(solution)/shard_map/ppermute | solution.py:288
  40.0 5.6 %collective-permute-start.1 = (bf16[2,16,1024]{2,1,0:T(8,128)(2,1)S(1)}, bf16[2,16,1024]{2,1,0:T(8,128)(2,1)S(1)}, u32[]{:S(2)}, u32[]{:S(2)}) collective-permute-start(bf16[2,16,1024]{2,1,0:T(8,128)(2,1)S(1)} %get-tuple-element.12), channel_id=1, source_target_pairs={{1,0},{2,1},{3,2},{4,3},{5,4},{6,5},{7,6},{8,7},{9,8},{10,9},{11,1... | collective-permute-start | bytes 196616 | tf_op jit(solution)/shard_map/ppermute | solution.py:289
  52.8 126.8 %all-gather.6.cloned.1.call-start = ((), (), s32[]{:S(2)}) async-start(), calls=%async_computation.1 | async-start | bytes 8912896 | tf_op jit(solution)/shard_map/all_gather | solution.py:35
  112.4 11.9 %slice-start = ((s8[12582912]{0:T(1024)(128)(4,1)}), s8[4194304]{0:T(1024)(128)(4,1)S(1)}, s32[]{:S(2)}) async-start(s8[12582912]{0:T(1024)(128)(4,1)} %bitcast.194), calls=%async_computation.2 | async-start | bytes 8388608
  117.8 6.5 %slice-start.1 = ((s8[12582912]{0:T(1024)(128)(4,1)}), s8[4194304]{0:T(1024)(128)(4,1)S(1)}, s32[]{:S(2)}) async-start(s8[12582912]{0:T(1024)(128)(4,1)} %bitcast.194), calls=%async_computation.3 | async-start | bytes 8388608
  117.8 6.5 %slice-start.2 = ((s8[12582912]{0:T(1024)(128)(4,1)}), s8[4194304]{0:T(1024)(128)(4,1)S(1)}, s32[]{:S(2)}) async-start(s8[12582912]{0:T(1024)(128)(4,1)} %bitcast.194), calls=%async_computation.4 | async-start | bytes 8388608
  194.5 6.3 %copy-start.2 = (bf16[1024,512]{1,0:T(8,128)(2,1)S(1)}, bf16[1024,512]{1,0:T(8,128)(2,1)}, u32[]{:S(2)}) copy-start(bf16[1024,512]{1,0:T(8,128)(2,1)} %param.27) | copy-start | bytes 3145732
  194.5 11.1 %copy-start.3 = (bf16[256,512]{1,0:T(8,128)(2,1)S(1)}, bf16[256,512]{1,0:T(8,128)(2,1)}, u32[]{:S(2)}) copy-start(bf16[256,512]{1,0:T(8,128)(2,1)} %param.20) | copy-start | bytes 786436
  194.5 11.1 %copy-start.4 = (bf16[512]{0:T(512)(128)(2,1)S(1)}, bf16[512]{0:T(512)(128)(2,1)}, u32[]{:S(2)}) copy-start(bf16[512]{0:T(512)(128)(2,1)} %param.28) | copy-start | bytes 3076
  201.1 4.5 %collective-permute-start.2 = (bf16[2,16,512]{2,1,0:T(8,128)(2,1)S(1)}, bf16[2,16,512]{2,1,0:T(8,128)(2,1)S(1)}, u32[]{:S(2)}, u32[]{:S(2)}) collective-permute-start(bf16[2,16,512]{2,1,0:T(8,128)(2,1)S(1)} %get-tuple-element.13), channel_id=1, source_target_pairs={{0,1},{1,2},{2,3},{3,4},{4,5},{5,6},{6,7},{7,8},{8,9},{9,10},{10,1... | collective-permute-start | bytes 98312 | tf_op jit(solution)/shard_map/ppermute | solution.py:294
  203.1 5.3 %collective-permute-start.3 = (bf16[2,16,512]{2,1,0:T(8,128)(2,1)S(1)}, bf16[2,16,512]{2,1,0:T(8,128)(2,1)S(1)}, u32[]{:S(2)}, u32[]{:S(2)}) collective-permute-start(bf16[2,16,512]{2,1,0:T(8,128)(2,1)S(1)} %get-tuple-element.14), channel_id=1, source_target_pairs={{1,0},{2,1},{3,2},{4,3},{5,4},{6,5},{7,6},{8,7},{9,8},{10,9},{11,1... | collective-permute-start | bytes 98312 | tf_op jit(solution)/shard_map/ppermute | solution.py:295
  209.5 143.4 %copy-start.1 = (bf16[1536,1024]{1,0:T(8,128)(2,1)S(1)}, bf16[1536,1024]{1,0:T(8,128)(2,1)}, u32[]{:S(2)}) copy-start(bf16[1536,1024]{1,0:T(8,128)(2,1)} %param.21) | copy-start | bytes 9437188
Sparse Core Ops, SparseCore 0:
  52.9 49.7 all-gather.3
  128.5 51.0 all-gather.5

commit v3 on v2

--- a/solution.py
+++ b/solution.py
@@ -28,17 +28,6 @@
 
 def fdot(lhs, rhs, dims=(((1,), (0,)), ((), ()))):
     return lax.dot_general(lhs, rhs, dims, preferred_element_type=jnp.float32)
-
-
-def attn_mlp_block(hidden, w_qkv, w_proj, w_up, w_down):
-    proj_qkv = jnp.einsum('cnd,dshk->scnhk', layer_norm(hidden), w_qkv, preferred_element_type=jnp.float32).astype(jnp.bfloat16)
-    kv_all = lax.all_gather(proj_qkv[1:], 'sp', axis=2, tiled=True)
-    scores = jnp.einsum('cqhk,cshk->chqs', proj_qkv[0], kv_all[0], preferred_element_type=jnp.float32) * proj_qkv.shape[-1] ** -0.5
-    attn_probs = jax.nn.softmax(scores, axis=-1).astype(jnp.bfloat16)
-    attended = jnp.einsum('chqs,cshk->cqhk', attn_probs, kv_all[1], preferred_element_type=jnp.float32).astype(jnp.bfloat16)
-    mid_state = (hidden + jnp.einsum('cqhk,hkd->cqd', attended, w_proj, preferred_element_type=jnp.float32)).astype(jnp.bfloat16)
-    up_act = jax.nn.gelu(jnp.einsum('cnd,df->cnf', layer_norm(mid_state), w_up, preferred_element_type=jnp.float32), approximate=False).astype(jnp.bfloat16)
-    return (mid_state + jnp.einsum('cnf,fd->cnd', up_act, w_down, preferred_element_type=jnp.float32)).astype(jnp.bfloat16)
 
 
 class RingGather:
@@ -265,39 +254,242 @@
     )(u, w_qkv, w_proj, w_up, w_down)
 
 
+def encoder_kernel(n_chips, n_heads, patches_hbm, mask_ref, epos_hbm, dpos_hbm, wpe_hbm, bias_ref, wqkv_hbm, wproj_hbm,
+                   wup_hbm, wdown_hbm, wed_hbm, token_ref, u_ref,
+                   patches, epos, dpos, wpe, wqkv, wproj, wup, wdown, wed,
+                   gath, kvt, q_ref, o_ref, hid, mx_ref, sel_ref, shift_ref, emb_ref, place_ref, edge_ref, z_ref, count_ref,
+                   send, recv, csend, crecv, esend, erecv, fsem, wsem):
+    n_clips, tokens, _ = u_ref.shape
+    n_layers, width = wproj.shape[0], wproj.shape[1]
+    size = 2 * n_chips
+    keep = hid.shape[0] // n_clips
+    half = keep // 2
+    slots = 2 * keep
+    head_dim = width // n_heads
+    lanes = 256
+    pack = lanes // head_dim
+    scale = head_dim ** -0.5 * LOG2E
+    bf, f32 = jnp.bfloat16, jnp.float32
+    ring = RingGather(n_chips, keep, gath, send, recv)
+    me = lax.axis_index('sp')
+
+    fetch = [pltpu.make_async_copy(src, dst, fsem.at[i]) for i, (src, dst) in enumerate(
+        ((patches_hbm, patches), (wpe_hbm, wpe), (epos_hbm, epos), (dpos_hbm, dpos), (wed_hbm, wed)))]
+    for copy in fetch:
+        copy.start()
+
+    def layer_copy(layer, i):
+        src = (wqkv_hbm, wproj_hbm, wup_hbm, wdown_hbm)[i].at[layer]
+        dst = (wqkv.at[layer], wproj.at[layer], wup, wdown)[i]
+        return pltpu.make_async_copy(src, dst, wsem.at[layer, i])
+
+    sem = pltpu.get_barrier_semaphore()
+
+    def greet(t, carry):
+        pl.semaphore_signal(sem, inc=1, device_id={'sp': lax.rem(me + t, size)}, device_id_type=MESH)
+        return carry
+
+    lax.fori_loop(1, size, greet, 0)
+
+    row_id = lax.broadcasted_iota(jnp.int32, (slots, tokens), 0).astype(f32)
+    earlier = (lax.broadcasted_iota(jnp.int32, (tokens, tokens), 0)
+               < lax.broadcasted_iota(jnp.int32, (tokens, tokens), 1)).astype(f32).astype(bf)
+    masks = [jnp.broadcast_to(mask_ref[c:c + 1, :].astype(f32), (8, tokens)) for c in range(n_clips)]
+    line = lax.broadcasted_iota(jnp.int32, (8, 128), 0)
+    mine = jnp.zeros((8, 128), f32)
+    occupied = []
+    for c in range(n_clips):
+        mine = jnp.where(line == c, jnp.sum(masks[c], axis=1, keepdims=True), mine)
+        rank = fdot(masks[c].astype(bf), earlier)
+        sel = jnp.where((row_id == rank[0:1]) & (masks[c][0:1] > 0.5), 1.0, 0.0)
+        occupied.append(jnp.sum(sel, axis=1, keepdims=True))
+        sel_ref[c] = sel.astype(bf)
+    count_ref[me] = mine
+    pl.semaphore_wait(sem, size - 1)
+
+    def count_copy(t):
+        return pltpu.make_async_remote_copy(
+            src_ref=count_ref.at[me], dst_ref=count_ref.at[me], send_sem=csend.at[t], recv_sem=crecv.at[t],
+            device_id={'sp': lax.rem(me + t, size)}, device_id_type=MESH)
+
+    def count_from(t):
+        src = lax.rem(me + size - t, size)
+        return pltpu.make_async_remote_copy(
+            src_ref=count_ref.at[src], dst_ref=count_ref.at[src], send_sem=csend.at[t], recv_sem=crecv.at[t],
+            device_id={'sp': lax.rem(me + t, size)}, device_id_type=MESH)
+
+    lax.fori_loop(1, size, lambda t, carry: (count_copy(t).start(), carry)[1], 0)
+    for copy in fetch[:3]:
+        copy.wait()
+    for i in range(4):
+        layer_copy(0, i).start()
+    for layer in range(1, n_layers):
+        for i in range(2):
+            layer_copy(layer, i).start()
+
+    for c in range(n_clips):
+        mx_ref[c * slots:(c + 1) * slots] = fdot(sel_ref[c], patches[c]).astype(bf)
+    embedded = fdot(mx_ref[...], wpe[...])
+    bias = bias_ref[...].astype(f32)
+    for c in range(n_clips):
+        emb_ref[c] = (embedded[c * slots:(c + 1) * slots] + occupied[c] * bias + fdot(sel_ref[c], epos[...])).astype(bf)
+
+    lax.fori_loop(1, size, lambda t, carry: (count_from(t).wait_recv(), carry)[1], 0)
+    source = lax.broadcasted_iota(jnp.int32, (size, 8, 128), 0)
+    offset = (half - me * keep).astype(f32) + jnp.sum(jnp.where(source < me, count_ref[...], 0.0), axis=0)
+    apart = (lax.broadcasted_iota(jnp.int32, (slots, slots), 0) - lax.broadcasted_iota(jnp.int32, (slots, slots), 1)).astype(f32)
+    for c in range(n_clips):
+        shift_ref[c] = jnp.where(apart == offset[c:c + 1, :slots], 1.0, 0.0).astype(bf)
+        place_ref[c] = fdot(shift_ref[c], emb_ref[c]).astype(bf)
+
+    after, before = lax.rem(me + 1, size), lax.rem(me + size - 1, size)
+
+    def edge_copy(i, src, dst, peer):
+        return pltpu.make_async_remote_copy(src_ref=src, dst_ref=dst, send_sem=esend.at[i], recv_sem=erecv.at[i],
+                                            device_id={'sp': peer}, device_id_type=MESH)
+
+    edges = [edge_copy(0, place_ref.at[:, pl.ds(slots - half, half)], edge_ref.at[0], after),
+             edge_copy(1, place_ref.at[:, pl.ds(0, half)], edge_ref.at[1], before)]
+    for copy in edges:
+        copy.start()
+    for copy in edges:
+        copy.wait_recv()
+    for c in range(n_clips):
+        for i in range(2):
+            hid[c * keep + i * half:c * keep + (i + 1) * half] = (
+                place_ref[c, half + i * half:half + (i + 1) * half].astype(f32) + edge_ref[i, c].astype(f32)).astype(bf)
+    gath[0, 0, 0] = layer_norm(hid[...])
+
+    block = (lax.broadcasted_iota(jnp.int32, (pack * keep, lanes), 0) // keep
+             == lax.broadcasted_iota(jnp.int32, (pack * keep, lanes), 1) // head_dim).astype(f32)
+    block_bf = block.astype(bf)
+    order = [0]
+    for i in range(1, n_chips // 2):
+        order += [i, n_chips - i]
+    order.append(n_chips // 2)
+    n_parts = 2
+    part = n_chips // n_parts
+    part_keys = part * 2 * keep
+
+    def layer_body(layer, carry):
+        ring.begin(layer)
+        layer_copy(layer, 0).wait()
+        q_ref[...] = fdot(gath[layer, 0, 0], wqkv[layer, :width], NT).astype(bf)
+        for i in range(n_parts):
+            picked = order[i * part:(i + 1) * part]
+            ready = ring.arrivals if i == n_parts - 1 else PIECES * (n_chips // 4)
+            done = 0 if i == 0 else PIECES * (n_chips // 4)
+            lax.fori_loop(done, ready, lambda k, carry: (ring.relay(layer, k), carry)[1], 0)
+            for slot in picked:
+                ring.take(layer, slot)
+            for c in range(n_clips):
+                a = jnp.concatenate([gath[layer, slot, :, c * keep:(c + 1) * keep].reshape(2 * keep, width) for slot in picked], axis=0)
+                kvt[c, :, i * part_keys:(i + 1) * part_keys] = fdot(wqkv[layer, width:], a, NT).astype(bf)
+
+        for c in range(n_clips):
+            for g in range(width // lanes):
+                at = slice(g * lanes, (g + 1) * lanes)
+                q = q_ref[c * keep:(c + 1) * keep, at]
+                s = fdot(jnp.concatenate([q] * pack, axis=0) * block_bf, kvt[c, at, :])
+                e = jnp.exp2((s - jnp.max(s, axis=1, keepdims=True)) * scale)
+                p = (e * (1.0 / jnp.sum(e, axis=1, keepdims=True))).astype(bf)
+                o = fdot(p, kvt[c, width + g * lanes:width + (g + 1) * lanes, :], NT) * block
+                total = o[:keep]
+                for h in range(1, pack):
+                    total = total + o[h * keep:(h + 1) * keep]
+                o_ref[c * keep:(c + 1) * keep, at] = total.astype(bf)
+
+        layer_copy(layer, 1).wait()
+        mid = (hid[...].astype(f32) + fdot(o_ref[...], wproj[layer])).astype(bf)
+        normed = layer_norm(mid)
+        down = mid.astype(f32)
+        layer_copy(layer, 2).wait()
+        layer_copy(layer, 3).wait()
+        for f in range(0, wup.shape[1], width):
+            act = gelu(fdot(normed, wup[:, f:f + width])).astype(bf)
+            down = down + fdot(act, wdown[f:f + width, :])
+        new = down.astype(bf)
+        hid[...] = new
+
+        @pl.when(layer + 1 < n_layers)
+        def _():
+            for i in (2, 3):
+                layer_copy(layer + 1, i).start()
+            gath[layer + 1, 0, 0] = layer_norm(new)
+
+        return carry
+
+    lax.fori_loop(0, n_layers, layer_body, 0)
+
+    for copy in fetch[3:]:
+        copy.wait()
+    z = fdot(layer_norm(hid[...]), wed[...]).astype(bf)
+    for c in range(n_clips):
+        z_ref[c, half:half + keep] = z[c * keep:(c + 1) * keep]
+    z_edges = [edge_copy(2, z_ref.at[:, pl.ds(keep, half)], z_ref.at[:, pl.ds(0, half)], after),
+               edge_copy(3, z_ref.at[:, pl.ds(half, half)], z_ref.at[:, pl.ds(half + keep, half)], before)]
+    for copy in z_edges:
+        copy.start()
+    first_line = lax.broadcasted_iota(jnp.int32, (8, tokens), 0) == 0
+    token = jnp.broadcast_to(token_ref[...].astype(f32), (8, token_ref.shape[1])).astype(bf)
+    hidden_part = [fdot(jnp.where(first_line, 1.0 - m, 0.0).astype(bf), token, TN) for m in masks]
+    for copy in z_edges:
+        copy.wait_recv()
+    for c in range(n_clips):
+        own = fdot(shift_ref[c], z_ref[c], TN).astype(bf)
+        u_ref[c] = (fdot(sel_ref[c], own, TN) + hidden_part[c] + dpos[...].astype(f32)).astype(bf)
+
+    lax.fori_loop(1, size, lambda t, carry: (count_copy(t).wait_send(), carry)[1], 0)
+    for copy in edges + z_edges:
+        copy.wait_send()
+    ring.drain(n_layers)
+
+
+def run_encoder(n_chips, patches, mask, enc_pos, dec_pos, w_pe, b_pe, w_qkv, w_proj, w_up, w_down, w_ed, token):
+    n_clips, tokens, patch = patches.shape
+    n_layers, width, _, n_heads, head_dim = w_qkv.shape
+    mlp, out_width = w_up.shape[2], w_ed.shape[1]
+    keep = tokens // KEEP_DIV
+    rows, slots = n_clips * keep, 2 * keep
+    bf, f32 = jnp.bfloat16, jnp.float32
+    w_qkv = jnp.transpose(w_qkv, (0, 2, 3, 4, 1)).reshape(n_layers, 3 * width, width)
+    w_proj = w_proj.reshape(n_layers, width, width)
+    vmem, hbm = pl.BlockSpec(memory_space=pltpu.VMEM), pl.BlockSpec(memory_space=pl.ANY)
+    dma = pltpu.SemaphoreType.DMA
+    keys = 2 * n_chips * keep
+    flops = 2 * n_layers * rows * width * (4 * width + 2 * mlp) + 4 * n_layers * keys * n_clips * width * width
+    return pl.pallas_call(
+        functools.partial(encoder_kernel, n_chips, n_heads),
+        out_shape=jax.ShapeDtypeStruct((n_clips, tokens, out_width), bf),
+        in_specs=[hbm, vmem, hbm, hbm, hbm, vmem, hbm, hbm, hbm, hbm, hbm, vmem],
+        out_specs=vmem,
+        scratch_shapes=[
+            pltpu.VMEM(patches.shape, bf), pltpu.VMEM(enc_pos.shape, bf), pltpu.VMEM(dec_pos.shape, bf),
+            pltpu.VMEM(w_pe.shape, bf), pltpu.VMEM(w_qkv.shape, bf), pltpu.VMEM(w_proj.shape, bf),
+            pltpu.VMEM(w_up.shape[1:], bf), pltpu.VMEM(w_down.shape[1:], bf), pltpu.VMEM(w_ed.shape, bf),
+            pltpu.VMEM((n_layers, n_chips, 2, rows, width), bf),
+            pltpu.VMEM((n_clips, 2 * width, keys), bf),
+            pltpu.VMEM((rows, width), bf), pltpu.VMEM((rows, width), bf), pltpu.VMEM((rows, width), bf),
+            pltpu.VMEM((n_clips * slots, patch), bf),
+            pltpu.VMEM((n_clips, slots, tokens), bf), pltpu.VMEM((n_clips, slots, slots), bf),
+            pltpu.VMEM((n_clips, slots, width), bf), pltpu.VMEM((n_clips, slots, width), bf),
+            pltpu.VMEM((2, n_clips, keep // 2, width), bf), pltpu.VMEM((n_clips, slots, out_width), bf),
+            pltpu.VMEM((2 * n_chips, 8, 128), f32),
+            dma((n_layers, 3, n_chips, PIECES)), dma((n_layers, 3, n_chips, PIECES)),
+            dma((2 * n_chips,)), dma((2 * n_chips,)), dma((4,)), dma((4,)), dma((5,)), dma((n_layers, 4)),
+        ],
+        compiler_params=pltpu.CompilerParams(collective_id=2, has_side_effects=True, vmem_limit_bytes=60 * 1024 * 1024),
+        cost_estimate=pl.CostEstimate(flops=flops, bytes_accessed=56 * 1024 * 1024, transcendentals=0),
+        name='encoder',
+    )(patches, mask, enc_pos, dec_pos, w_pe, b_pe.reshape(1, -1), w_qkv, w_proj, w_up, w_down, w_ed, token.reshape(1, -1))
+
+
 def solution(mesh):
-    group_size = mesh.shape['sp']
-    to_next = [(src_dev, src_dev + 1) for src_dev in range(group_size - 1)]
-    to_prev = [(src_dev + 1, src_dev) for src_dev in range(group_size - 1)]
+    n_chips = mesh.shape['sp'] // 2
 
     def local_program(patches, vis_mask, enc_pos, dec_pos, w_pe, b_pe, enc_qkv, enc_proj, enc_up, enc_down, w_ed, mask_token, dec_qkv, dec_proj, dec_up, dec_down, w_out):
-        vis_shard = patches.shape[1] // KEEP_DIV
-        half_rows = vis_shard // 2
-        my_index = lax.axis_index('sp')
-        vis_counts = lax.all_gather(jnp.sum(vis_mask, axis=1), 'sp')
-        vis_before = jnp.sum(jnp.where(jnp.arange(group_size)[:, None] < my_index, vis_counts, 0), axis=0)
-        local_rank = jnp.cumsum(vis_mask, axis=1) - vis_mask
-        dest_row = vis_before[:, None] + local_rank - my_index * vis_shard + half_rows
-        row_ids = jnp.arange(2 * vis_shard)
-        select = ((dest_row[:, None, :] == row_ids[None, :, None]) & (vis_mask[:, None, :] == 1)).astype(jnp.bfloat16)
-        moved_x = jnp.einsum('cqi,cip->cqp', select, patches, preferred_element_type=jnp.float32).astype(jnp.bfloat16)
-        moved_pos = jnp.einsum('cqi,id->cqd', select, enc_pos, preferred_element_type=jnp.float32)
-        occupied = jnp.sum(select, axis=2, dtype=jnp.float32)
-        embedded = (jnp.einsum('cqp,pd->cqd', moved_x, w_pe, preferred_element_type=jnp.float32)
-                    + occupied[:, :, None] * b_pe.astype(jnp.float32) + moved_pos).astype(jnp.bfloat16)
-        from_prev = lax.ppermute(embedded[:, 3 * half_rows:], 'sp', to_next)
-        from_next = lax.ppermute(embedded[:, :half_rows], 'sp', to_prev)
-        hidden = embedded[:, half_rows:3 * half_rows] + jnp.concatenate([from_prev, from_next], axis=1)
-        for layer_idx in range(enc_qkv.shape[0]):
-            hidden = attn_mlp_block(hidden, enc_qkv[layer_idx], enc_proj[layer_idx], enc_up[layer_idx], enc_down[layer_idx])
-        z_enc = jnp.einsum('cnd,de->cne', layer_norm(hidden), w_ed, preferred_element_type=jnp.float32).astype(jnp.bfloat16)
-        z_prev = lax.ppermute(z_enc[:, half_rows:], 'sp', to_next)
-        z_next = lax.ppermute(z_enc[:, :half_rows], 'sp', to_prev)
-        z_rows = jnp.concatenate([z_prev, z_enc, z_next], axis=1)
-        placed = jnp.einsum('cqi,cqe->cie', select, z_rows, preferred_element_type=jnp.float32)
-        masked_part = (1 - vis_mask).astype(jnp.float32)[:, :, None] * mask_token.astype(jnp.float32)
-        hidden = (placed + masked_part + dec_pos.astype(jnp.float32)).astype(jnp.bfloat16)
-        hidden = run_decoder(group_size // 2, hidden, dec_qkv, dec_proj, dec_up, dec_down)
+        hidden = run_encoder(n_chips, patches, vis_mask, enc_pos, dec_pos, w_pe, b_pe, enc_qkv, enc_proj, enc_up, enc_down, w_ed, mask_token)
+        hidden = run_decoder(n_chips, hidden, dec_qkv, dec_proj, dec_up, dec_down)
         return jnp.einsum('cne,ep->cnp', layer_norm(hidden), w_out, preferred_element_type=jnp.float32)
 
     row_spec = P('dp', 'sp', None)

time: 360 us -> 223 us (0.62)
  waiting for transfers between devices: 108 us -> 0 us
  Pallas kernels: 137 us -> 213 us
  matrix products: 59.9 us -> 3.73 us
  blocking collectives: 16.1 us -> 0 us
  between operations: 14.4 us -> 0.04 us
  starting transfers between devices: 11.9 us -> 0 us
  other arithmetic: 9.08 us -> 2.53 us
    all_gather x2 -> x0, waiting for transfers between devices: 101 us -> none  [attn_mlp_block(): kv_all = lax.all_gather(proj_qkv[1:], 'sp', axis=2, tiled=True)]
    pallas_call x0 -> x1, Pallas kernels: none -> 76.3 us  [run_encoder(): pl.pallas_call(functools.partial(encoder_kernel, n_chips, n_heads), out_s...]
    dot_general x14 -> x0, matrix products: 55.6 us -> none  [the longest x2 12.3 us: attn_mlp_block(): jnp.einsum('cnf,fd->cnd', up_act, w_down, preferred_element_type=jnp.floa...]
    unnamed x1 -> x0, blocking collectives: 16.1 us -> none
    ppermute x4 -> x0, starting transfers between devices: 11.8 us -> none  [the longest x1 5.45 us: local_program(): from_prev = lax.ppermute(embedded[:, 3 * half_rows:], 'sp', to_next)]
    ppermute x4 -> x0, waiting for transfers between devices: 6.37 us -> none  [the longest x1 3.65 us: local_program(): from_next = lax.ppermute(embedded[:, :half_rows], 'sp', to_prev)]
  transfers between devices with their start and end apart: 6 -> 0, of which waited for: 4 -> 0; matrix products, arithmetic and copies ran while one was open for 0% -> 0% of each run, Pallas kernels for 0% -> 0%
where the time goes in v3:
time: 223 us; the launch traced here: 222 us
  Pallas kernels  213 us (96%)
  matrix products  3.73 us (2%)
  local copies, waits for them, and re-layouts  2.67 us (1%)
  other arithmetic  2.53 us (1%)
    pallas_call x1, Pallas kernels, run_decoder(): pl.pallas_call(functools.partial(decoder_kernel, n_chips, n_heads), out_s...  137 us
    pallas_call x1, Pallas kernels, run_encoder(): pl.pallas_call(functools.partial(encoder_kernel, n_chips, n_heads), out_s...  76.3 us

profile of v3, /device:TPU:21, one launch (start us, length us, event | category | flops | bytes accessed | tf_op | source)
XLA Modules:
  0.0 222.4 jit_solution(8226736453279625871)
XLA Ops:
  0.0 0.0 copy-start
  0.0 1.4 reshape.33.token_ref
  1.4 1.3 reshape.30.bias_ref
  2.7 76.3 %encoder.1.u_ref = bf16[2,256,512]{2,1,0:T(8,128)(2,1)} custom-call(bf16[2,256,1536]{2,1,0:T(8,128)(2,1)} %patches_hbm.1, s32[2,256]{1,0:T(2,128)} %mask_ref.1, bf16[256,1024]{1,0:T(8,128)(2,1)} %epos_hbm.1, bf16[256,512]{1,0:T(8,128)(2,1)} %dpos_hbm.1, bf16[1536,1024]{1,0:T(8,128)(2,1)} %wpe_hbm.1, bf16[1,1024]{1,0:T(2,128)(2,1)} %reshape.30.bias_ref, ...), custom_call_target="tpu_custom_call" | custom-call | flops 11811160064 | bytes 58720256 | tf_op jit(solution)/shard_map/encoder/pallas_call | solution.py:461
  79.0 137.1 %decoder.1 = bf16[2,256,512]{2,1,0:T(8,128)(2,1)} custom-call(bf16[2,256,512]{2,1,0:T(8,128)(2,1)} %encoder.1.u_ref, bf16[2,3,512,512]{3,2,1,0:T(8,128)(2,1)} %bitcast.13, bf16[2,512,512]{2,1,0:T(8,128)(2,1)} %bitcast.14, bf16[2,512,2048]{2,1,0:T(8,128)(2,1)} %wup_hbm.3, bf16[2,2048,512]{2,1,0:T(8,128)(2,1)} %wdown_hbm.3), custom_call_target="tpu_custom_call" | custom-call | flops 38654705664 | bytes 16777216 | tf_op jit(solution)/shard_map/decoder/pallas_call | solution.py:229
  216.1 1.2 convert_reduce_fusion
  217.3 1.3 fusion.4
  218.6 0.0 copy-done
  218.6 3.7 %fusion = f32[2,256,1536]{2,1,0:T(8,128)} fusion(bf16[512,1536]{1,0:T(8,128)(2,1)S(1)} %copy-done, bf16[2,256,512]{2,1,0:T(8,128)(2,1)} %decoder.1, f32[2,256]{1,0:T(2,128)S(1)} %add_rsqrt_fusion, f32[2,256]{1,0:T(2,128)S(1)} %broadcast_multiply_fusion), kind=kOutput, calls=%fused_computation | convolution fusion | flops 806354944 | bytes 5246976 | tf_op jit(solution)/shard_map/cne,ep->cnp/dot_general | solution.py:493
  (2 shorter events, 0.0 us)
Async XLA Ops:
  0.0 218.6 %copy-start = (bf16[512,1536]{1,0:T(8,128)(2,1)S(1)}, bf16[512,1536]{1,0:T(8,128)(2,1)}, u32[]{:S(2)}) copy-start(bf16[512,1536]{1,0:T(8,128)(2,1)} %param.33) | copy-start | bytes 4718596

commit v4 on v3

--- a/solution.py
+++ b/solution.py
@@ -8,7 +8,8 @@
 from jax.sharding import PartitionSpec as P
 
 KEEP_DIV = 8
-PIECES = 2
+ENC_PIECES = 2
+DEC_PIECES = 2
 MESH = pl.DeviceIdType.MESH
 LOG2E = 1.4426950408889634
 NT = (((1,), (1,)), ((), ()))
@@ -31,14 +32,15 @@
 
 
 class RingGather:
-    def __init__(self, n_chips, piece_rows, buf, send, recv):
-        self.n, self.rows, self.buf, self.send, self.recv = n_chips, piece_rows, buf, send, recv
+    def __init__(self, n_chips, pieces, buf, send, recv):
+        self.n, self.pieces, self.buf, self.send, self.recv = n_chips, pieces, buf, send, recv
+        self.rows = buf.shape[3] // pieces
         me = lax.axis_index('sp')
         size = 2 * n_chips
         self.right = lax.rem(me + 2, size)
         self.left = lax.rem(me + size - 2, size)
         self.mate = me + 1 - 2 * lax.rem(me, 2)
-        self.arrivals = PIECES * (n_chips // 2) - 1
+        self.arrivals = pieces * (n_chips // 2 - 1) + pieces // 2
 
     def barrier(self):
         sem = pltpu.get_barrier_semaphore()
@@ -60,44 +62,47 @@
             device_id={'sp': peer}, device_id_type=MESH)
 
     def begin(self, phase):
-        for piece in range(PIECES):
+        for piece in range(self.pieces):
             self.copy(phase, 0, 0, piece).start()
-            self.copy(phase, 1, 0, PIECES - 1 - piece).start()
+            self.copy(phase, 1, 0, self.pieces - 1 - piece).start()
             self.copy(phase, 2, 0, piece).start()
 
     def relay(self, phase, k):
-        step = k // PIECES
-        p_right = lax.rem(k, PIECES)
-        p_left = PIECES - 1 - p_right
+        step = k // self.pieces
+        p_right = lax.rem(k, self.pieces)
+        p_left = self.pieces - 1 - p_right
         self.copy(phase, 0, step, p_right).wait_recv()
-        pl.when(k < self.arrivals - PIECES)(lambda: self.copy(phase, 0, step + 1, p_right).start())
+        pl.when(k < self.arrivals - self.pieces)(lambda: self.copy(phase, 0, step + 1, p_right).start())
         self.copy(phase, 2, step + 1, p_right).start()
         self.copy(phase, 1, step, p_left).wait_recv()
-        pl.when(k < self.arrivals - PIECES)(lambda: self.copy(phase, 1, step + 1, p_left).start())
+        pl.when(k < self.arrivals - self.pieces)(lambda: self.copy(phase, 1, step + 1, p_left).start())
         self.copy(phase, 2, self.n - 1 - step, p_left).start()
 
+    def relay_range(self, phase, low, high):
+        lax.fori_loop(low, high, lambda k, carry: (self.relay(phase, k), carry)[1], 0)
+
     def take(self, phase, slot):
-        for piece in range(PIECES):
+        for piece in range(self.pieces):
             self.copy(phase, 2, slot, piece).wait_recv()
 
     def drain(self, phases):
         def per_slot(i, carry):
-            slot = lax.rem(i // PIECES, self.n)
-            self.copy(i // (PIECES * self.n), 2, slot, lax.rem(i, PIECES)).wait_send()
+            slot = lax.rem(i // self.pieces, self.n)
+            self.copy(i // (self.pieces * self.n), 2, slot, lax.rem(i, self.pieces)).wait_send()
             return carry
 
         def per_hop(i, carry):
             phase, k = i // self.arrivals, lax.rem(i, self.arrivals)
-            self.copy(phase, 0, k // PIECES, lax.rem(k, PIECES)).wait_send()
-            self.copy(phase, 1, k // PIECES, PIECES - 1 - lax.rem(k, PIECES)).wait_send()
+            self.copy(phase, 0, k // self.pieces, lax.rem(k, self.pieces)).wait_send()
+            self.copy(phase, 1, k // self.pieces, self.pieces - 1 - lax.rem(k, self.pieces)).wait_send()
             return carry
 
-        lax.fori_loop(0, phases * PIECES * self.n, per_slot, 0)
+        lax.fori_loop(0, phases * self.pieces * self.n, per_slot, 0)
         lax.fori_loop(0, phases * self.arrivals, per_hop, 0)
 
 
 def decoder_kernel(n_chips, n_heads, u_ref, wqkv_hbm, wproj_hbm, wup_hbm, wdown_hbm, state,
-                   gath, k_ref, vt_ref, s_even, s_odd, m_ref, qm_ref, ot_ref, wqkv, wproj, wup, wdown, send, recv, wsem):
+                   gath, k_ref, vt_ref, s_even, s_odd, m_ref, qm_ref, ot_ref, acc_ref, sum_ref, top_ref, wqkv, wproj, wup, wdown, send, recv, wsem):
     n_clips, rows, width = u_ref.shape
     n_layers = wproj.shape[0]
     phases = n_layers * n_clips
@@ -106,7 +111,7 @@
     chunk = 2 * rows
     scale = head_dim ** -0.5 * LOG2E
     s_both = (s_even, s_odd)
-    ring = RingGather(n_chips, rows // PIECES, gath, send, recv)
+    ring = RingGather(n_chips, DEC_PIECES, gath, send, recv)
 
     weights = [pltpu.make_async_copy(src, dst, wsem.at[i]) for i, (src, dst) in enumerate(
         ((wqkv_hbm, wqkv), (wproj_hbm, wproj), (wup_hbm, wup), (wdown_hbm, wdown)))]
@@ -121,9 +126,9 @@
     for copy in weights:
         copy.wait()
 
-    def scores(head, j, slot, top):
+    def scores(head, base, j, slot, top):
         group = head // lane_heads
-        keys = k_ref[j, :, pl.ds(pl.multiple_of(group * qm_ref.shape[1], qm_ref.shape[1]), qm_ref.shape[1])]
+        keys = k_ref[base + j, :, pl.ds(pl.multiple_of(group * qm_ref.shape[1], qm_ref.shape[1]), qm_ref.shape[1])]
         s = fdot(keys, qm_ref[head]).reshape(chunk // 8, 8, rows)
         s_both[slot][j] = s
         return jnp.maximum(top, jnp.max(s, axis=0))
@@ -131,71 +136,76 @@
     def set_top(slot, top):
         m_ref[slot] = jnp.broadcast_to(jnp.max(top, axis=0, keepdims=True), top.shape)
 
-    def values(head, j, slot, total, acc):
+    def values(head, base, j, slot, total, acc):
         e = jnp.exp2((s_both[slot][j] - m_ref[slot][None]) * scale)
-        vt = vt_ref[j, pl.ds(pl.multiple_of(head * head_dim, head_dim), head_dim), :]
+        vt = vt_ref[base + j, pl.ds(pl.multiple_of(head * head_dim, head_dim), head_dim), :]
         return total + jnp.sum(e, axis=0), acc + fdot(vt, e.reshape(chunk, rows).astype(jnp.bfloat16))
 
-    def put_out(head, total, acc):
-        out = acc * (1.0 / jnp.sum(total, axis=0, keepdims=True))
-        ot_ref[pl.ds(pl.multiple_of(head * head_dim, head_dim), head_dim), :] = out.astype(jnp.bfloat16)
-
-    low = jnp.full((8, rows), -jnp.inf, jnp.float32)
+    def head_rows(head):
+        return pl.ds(pl.multiple_of(head * head_dim, head_dim), head_dim)
+
+    def put_out(head, slot, total, acc):
+        ot_ref[head_rows(head), :] = (acc * (1.0 / jnp.sum(total, axis=0, keepdims=True))).astype(jnp.bfloat16)
+
+    def put_first(head, slot, total, acc):
+        top_ref[head] = m_ref[slot]
+        sum_ref[head] = total
+        acc_ref[head_rows(head), :] = acc
+
+    def put_second(head, slot, total, acc):
+        old, new = top_ref[head], m_ref[slot]
+        top = jnp.maximum(old, new)
+        keep_old, keep_new = jnp.exp2((old - top) * scale), jnp.exp2((new - top) * scale)
+        put_out(head, slot, sum_ref[head] * keep_old + total * keep_new,
+                acc_ref[head_rows(head), :] * keep_old[0:1] + acc * keep_new[0:1])
+
+    lowest = jnp.full((8, rows), -jnp.inf, jnp.float32)
     none = jnp.zeros((8, rows), jnp.float32)
     zero = jnp.zeros((head_dim, rows), jnp.float32)
-
-    def phase_body(phase, carry):
-        clip = lax.rem(phase, n_clips)
-        layer = phase // n_clips
-        more = phase + 1 < phases
-        first = phase == 0
-        pl.when(more & (phase > 0))(lambda: ring.begin(phase + 1))
-
-        def project(i, carry):
-            odd = lax.rem(i, 2)
-            r = jnp.where(odd == 1, (i + 1) // 2, lax.rem(n_chips - i // 2, n_chips))
-            pl.when(first & (odd == 1))(lambda: ring.relay(phase, i - 1))
-            pl.when(first & (odd == 1) & (i < ring.arrivals))(lambda: ring.relay(phase, i))
-            pl.when(more & first & (i == ring.arrivals - 1))(lambda: ring.begin(phase + 1))
-            ring.take(phase, r)
-            a = gath[phase, r].reshape(chunk, width)
-            k_ref[r] = fdot(a, wqkv[layer, 1], NT).astype(jnp.bfloat16)
-            vt_ref[r] = fdot(wqkv[layer, 2], a, NT).astype(jnp.bfloat16)
+    half_chips = n_chips // 2
+    assert ring.arrivals == 7 and n_heads == 16
+
+    def sweep(base, count, put, between):
+        top = lowest
+        for j in range(count):
+            top = scores(0, base, j, 0, top)
+        set_top(0, top)
+
+        def head_step(head, now, last=False):
+            top, total, acc = lowest, none, zero
+            for j in range(count):
+                if not last:
+                    top = scores(head + 1, base, j, 1 - now, top)
+                total, acc = values(head, base, j, now, total, acc)
+            if not last:
+                set_top(1 - now, top)
+            put(head, now, total, acc)
+
+        def head_pair(pair, carry):
+            between(pair)
+            head_step(2 * pair, 0)
+            head_step(2 * pair + 1, 1)
             return carry
 
-        lax.fori_loop(0, n_chips, project, 0)
+        lax.fori_loop(0, n_heads // 2 - 1, head_pair, 0)
+        between(jnp.int32(n_heads // 2 - 1))
+        head_step(n_heads - 2, 0)
+        head_step(n_heads - 1, 1, last=True)
+
+    def queries(phase, layer):
         qt = fdot(wqkv[layer, 0], gath[phase, 0, 0], NT).astype(jnp.bfloat16)
         for head in range(n_heads):
             at = (head % lane_heads) * head_dim
             qm_ref[head, at:at + head_dim, :] = qt[head * head_dim:(head + 1) * head_dim]
 
-        top = low
-        for j in range(n_chips):
-            top = scores(0, j, 0, top)
-        set_top(0, top)
-
-        def head_step(head, now, last=False):
-            top, total, acc = low, none, zero
-            for j in range(n_chips):
-                if not last:
-                    top = scores(head + 1, j, 1 - now, top)
-                total, acc = values(head, j, now, total, acc)
-            if not last:
-                set_top(1 - now, top)
-            put_out(head, total, acc)
-
-        def head_pair(pair, carry):
-            late = (pair > 2).astype(jnp.int32) + (pair > 5).astype(jnp.int32)
-            pl.when(more & (pair != 2) & (pair != 5))(lambda: ring.relay(phase + 1, pair - late))
-            head_step(2 * pair, 0)
-            head_step(2 * pair + 1, 1)
-            return carry
-
-        lax.fori_loop(0, n_heads // 2 - 1, head_pair, 0)
-        pl.when(more)(lambda: ring.relay(phase + 1, ring.arrivals - 2))
-        head_step(n_heads - 2, 0)
-        head_step(n_heads - 1, 1, last=True)
-
+    def project(phase, layer, i):
+        r = jnp.where(lax.rem(i, 2) == 1, (i + 1) // 2, lax.rem(n_chips - i // 2, n_chips))
+        ring.take(phase, r)
+        a = gath[phase, r].reshape(chunk, width)
+        k_ref[i] = fdot(a, wqkv[layer, 1], NT).astype(jnp.bfloat16)
+        vt_ref[i] = fdot(wqkv[layer, 2], a, NT).astype(jnp.bfloat16)
+
+    def complete(phase, layer, clip):
         mid = (state[clip].astype(jnp.float32) + fdot(ot_ref[...], wproj[layer], TN)).astype(jnp.bfloat16)
         normed = layer_norm(mid)
         down = mid.astype(jnp.float32)
@@ -209,10 +219,60 @@
         def _():
             gath[phase + n_clips, 0, 0] = layer_norm(new)
 
+        @pl.when(phase + n_clips >= phases)
+        def _():
+            state[clip] = layer_norm(new)
+
+
+    def opening(i, carry):
+        pl.when(lax.rem(i, 2) == 1)(lambda: ring.relay_range(0, i - 1, i + 1))
+        project(0, 0, i)
+        return carry
+
+    def rest(i, carry):
+        project(0, 0, i)
+        return carry
+
+    def between_first(pair):
+        pl.when((pair == 1) | (pair == 3) | (pair == 5))(lambda: ring.relay(0, half_chips + pair // 2))
+        pl.when(pair == 3)(lambda: ring.begin(1))
+
+    def between_second(pair):
+        pl.when((pair == 0) | (pair == 3) | (pair == 5) | (pair == 7))(lambda: ring.relay(1, pair // 2))
+
+    queries(0, 0)
+    lax.fori_loop(0, half_chips, opening, 0)
+    sweep(0, half_chips, put_first, between_first)
+    lax.fori_loop(half_chips, n_chips, rest, 0)
+    sweep(half_chips, half_chips, put_second, between_second)
+    complete(0, 0, 0)
+    ring.relay(1, half_chips)
+
+    def phase_body(phase, carry):
+        clip = lax.rem(phase, n_clips)
+        layer = phase // n_clips
+        more = phase + 1 < phases
+        pl.when(more & (phase > 1))(lambda: ring.begin(phase + 1))
+
+        def project_all(i, carry):
+            pl.when((phase == 1) & (i == 5))(lambda: ring.relay(phase, 5))
+            pl.when((phase == 1) & (i == 7))(lambda: ring.relay(phase, 6))
+            pl.when(more & (phase == 1) & (i == 6))(lambda: ring.begin(phase + 1))
+            project(phase, layer, i)
+            return carry
+
+        def between(pair):
+            late = (pair > 2).astype(jnp.int32) + (pair > 5).astype(jnp.int32)
+            pl.when(more & (pair != 2) & (pair != 5))(lambda: ring.relay(phase + 1, pair - late))
+
+        lax.fori_loop(0, n_chips, project_all, 0)
+        queries(phase, layer)
+        sweep(0, n_chips, put_out, between)
+        complete(phase, layer, clip)
         pl.when(more)(lambda: ring.relay(phase + 1, ring.arrivals - 1))
         return carry
 
-    lax.fori_loop(0, phases, phase_body, 0)
+    lax.fori_loop(1, phases, phase_body, 0)
     ring.drain(phases)
 
 
@@ -240,12 +300,15 @@
             pltpu.VMEM((2, 8, rows), jnp.float32),
             pltpu.VMEM((n_heads, 256, rows), bf),
             pltpu.VMEM((width, rows), bf),
+            pltpu.VMEM((width, rows), jnp.float32),
+            pltpu.VMEM((n_heads, 8, rows), jnp.float32),
+            pltpu.VMEM((n_heads, 8, rows), jnp.float32),
             pltpu.VMEM((n_layers, 3, width, width), bf),
             pltpu.VMEM((n_layers, width, width), bf),
             pltpu.VMEM((n_layers, width, mlp), bf),
             pltpu.VMEM((n_layers, mlp, width), bf),
-            pltpu.SemaphoreType.DMA((phases, 3, n_chips, PIECES)),
-            pltpu.SemaphoreType.DMA((phases, 3, n_chips, PIECES)),
+            pltpu.SemaphoreType.DMA((phases, 3, n_chips, DEC_PIECES)),
+            pltpu.SemaphoreType.DMA((phases, 3, n_chips, DEC_PIECES)),
             pltpu.SemaphoreType.DMA((4,)),
         ],
         compiler_params=pltpu.CompilerParams(collective_id=1, has_side_effects=True, vmem_limit_bytes=60 * 1024 * 1024),
@@ -270,7 +333,7 @@
     pack = lanes // head_dim
     scale = head_dim ** -0.5 * LOG2E
     bf, f32 = jnp.bfloat16, jnp.float32
-    ring = RingGather(n_chips, keep, gath, send, recv)
+    ring = RingGather(n_chips, ENC_PIECES, gath, send, recv)
     me = lax.axis_index('sp')
 
     fetch = [pltpu.make_async_copy(src, dst, fsem.at[i]) for i, (src, dst) in enumerate(
@@ -330,7 +393,7 @@
     for c in range(n_clips):
         mx_ref[c * slots:(c + 1) * slots] = fdot(sel_ref[c], patches[c]).astype(bf)
     embedded = fdot(mx_ref[...], wpe[...])
-    bias = bias_ref[...].astype(f32)
+    bias = bias_ref[...].astype(f32).reshape(1, width)
     for c in range(n_clips):
         emb_ref[c] = (embedded[c * slots:(c + 1) * slots] + occupied[c] * bias + fdot(sel_ref[c], epos[...])).astype(bf)
 
@@ -377,12 +440,15 @@
         q_ref[...] = fdot(gath[layer, 0, 0], wqkv[layer, :width], NT).astype(bf)
         for i in range(n_parts):
             picked = order[i * part:(i + 1) * part]
-            ready = ring.arrivals if i == n_parts - 1 else PIECES * (n_chips // 4)
-            done = 0 if i == 0 else PIECES * (n_chips // 4)
-            lax.fori_loop(done, ready, lambda k, carry: (ring.relay(layer, k), carry)[1], 0)
+            edge = ring.pieces * (n_chips // 4)
+            ready = ring.arrivals if i == n_parts - 1 else edge
+            done = 0 if i == 0 else edge + ring.pieces // 2 + 1
+            ring.relay_range(layer, done, ready)
             for slot in picked:
                 ring.take(layer, slot)
             for c in range(n_clips):
+                if i == 0 and c == 1:
+                    ring.relay_range(layer, edge, edge + ring.pieces // 2 + 1)
                 a = jnp.concatenate([gath[layer, slot, :, c * keep:(c + 1) * keep].reshape(2 * keep, width) for slot in picked], axis=0)
                 kvt[c, :, i * part_keys:(i + 1) * part_keys] = fdot(wqkv[layer, width:], a, NT).astype(bf)
 
@@ -431,7 +497,7 @@
     for copy in z_edges:
         copy.start()
     first_line = lax.broadcasted_iota(jnp.int32, (8, tokens), 0) == 0
-    token = jnp.broadcast_to(token_ref[...].astype(f32), (8, token_ref.shape[1])).astype(bf)
+    token = jnp.broadcast_to(token_ref[...].astype(f32).reshape(1, token_ref.shape[0]), (8, token_ref.shape[0])).astype(bf)
     hidden_part = [fdot(jnp.where(first_line, 1.0 - m, 0.0).astype(bf), token, TN) for m in masks]
     for copy in z_edges:
         copy.wait_recv()
@@ -475,13 +541,13 @@
             pltpu.VMEM((n_clips, slots, width), bf), pltpu.VMEM((n_clips, slots, width), bf),
             pltpu.VMEM((2, n_clips, keep // 2, width), bf), pltpu.VMEM((n_clips, slots, out_width), bf),
             pltpu.VMEM((2 * n_chips, 8, 128), f32),
-            dma((n_layers, 3, n_chips, PIECES)), dma((n_layers, 3, n_chips, PIECES)),
+            dma((n_layers, 3, n_chips, ENC_PIECES)), dma((n_layers, 3, n_chips, ENC_PIECES)),
             dma((2 * n_chips,)), dma((2 * n_chips,)), dma((4,)), dma((4,)), dma((5,)), dma((n_layers, 4)),
         ],
         compiler_params=pltpu.CompilerParams(collective_id=2, has_side_effects=True, vmem_limit_bytes=60 * 1024 * 1024),
         cost_estimate=pl.CostEstimate(flops=flops, bytes_accessed=56 * 1024 * 1024, transcendentals=0),
         name='encoder',
-    )(patches, mask, enc_pos, dec_pos, w_pe, b_pe.reshape(1, -1), w_qkv, w_proj, w_up, w_down, w_ed, token.reshape(1, -1))
+    )(patches, mask, enc_pos, dec_pos, w_pe, b_pe, w_qkv, w_proj, w_up, w_down, w_ed, token)
 
 
 def solution(mesh):
@@ -490,7 +556,7 @@
     def local_program(patches, vis_mask, enc_pos, dec_pos, w_pe, b_pe, enc_qkv, enc_proj, enc_up, enc_down, w_ed, mask_token, dec_qkv, dec_proj, dec_up, dec_down, w_out):
         hidden = run_encoder(n_chips, patches, vis_mask, enc_pos, dec_pos, w_pe, b_pe, enc_qkv, enc_proj, enc_up, enc_down, w_ed, mask_token)
         hidden = run_decoder(n_chips, hidden, dec_qkv, dec_proj, dec_up, dec_down)
-        return jnp.einsum('cne,ep->cnp', layer_norm(hidden), w_out, preferred_element_type=jnp.float32)
+        return jnp.einsum('cne,ep->cnp', hidden, w_out, preferred_element_type=jnp.float32)
 
     row_spec = P('dp', 'sp', None)
     pos_spec = P(('dp', 'sp'), None)

time: 223 us -> 218 us (0.978)
  local copies, waits for them, and re-layouts: 2.67 us -> 0.01 us
  other arithmetic: 2.53 us -> 0 us
    reshape x2 -> x0, local copies, waits for them, and re-layouts: 2.67 us -> none  [the longest x1 1.39 us: run_encoder(): token.reshape(1, -1)]
    reduce_sum x2 -> x0, other arithmetic: 2.51 us -> none  [the longest x1 1.32 us: layer_norm(): row_var = jnp.mean(centred * centred, axis=-1, keepdims=True)]
where the time goes in v4:
time: 218 us
  Pallas kernels  214 us (98%)
  matrix products  3.69 us (2%)
    pallas_call x1, Pallas kernels, run_decoder(): pl.pallas_call(functools.partial(decoder_kernel, n_chips, n_heads), out_s...  137 us
    pallas_call x1, Pallas kernels, run_encoder(): pl.pallas_call(functools.partial(encoder_kernel, n_chips, n_heads), out_s...  77.2 us

profile of v4, /device:TPU:21, one launch (start us, length us, event | category | flops | bytes accessed | tf_op | source)
XLA Modules:
  0.0 217.9 jit_solution(13742220694668664292)
XLA Ops:
  0.0 0.0 copy-start
  0.0 77.2 %encoder.1.u_ref = bf16[2,256,512]{2,1,0:T(8,128)(2,1)} custom-call(bf16[2,256,1536]{2,1,0:T(8,128)(2,1)} %patches_hbm.1, s32[2,256]{1,0:T(2,128)} %mask_ref.1, bf16[256,1024]{1,0:T(8,128)(2,1)} %epos_hbm.1, bf16[256,512]{1,0:T(8,128)(2,1)} %dpos_hbm.1, bf16[1536,1024]{1,0:T(8,128)(2,1)} %wpe_hbm.1, bf16[1024]{0:T(1024)(128)(2,1)} %bias_ref.1, ...), custom_call_target="tpu_custom_call" | custom-call | flops 11811160064 | bytes 58720256 | tf_op jit(solution)/shard_map/encoder/pallas_call | solution.py:527
  77.2 137.0 %decoder.1 = bf16[2,256,512]{2,1,0:T(8,128)(2,1)} custom-call(bf16[2,256,512]{2,1,0:T(8,128)(2,1)} %encoder.1.u_ref, bf16[2,3,512,512]{3,2,1,0:T(8,128)(2,1)} %bitcast.14, bf16[2,512,512]{2,1,0:T(8,128)(2,1)} %bitcast.15, bf16[2,512,2048]{2,1,0:T(8,128)(2,1)} %wup_hbm.3, bf16[2,2048,512]{2,1,0:T(8,128)(2,1)} %wdown_hbm.3), custom_call_target="tpu_custom_call" | custom-call | flops 38654705664 | bytes 16777216 | tf_op jit(solution)/shard_map/decoder/pallas_call | solution.py:289
  214.2 0.0 copy-done
  214.2 3.7 %fusion = f32[2,256,1536]{2,1,0:T(8,128)} fusion(bf16[2,256,512]{2,1,0:T(8,128)(2,1)} %decoder.1, bf16[512,1536]{1,0:T(8,128)(2,1)S(1)} %copy-done), kind=kOutput, calls=%fused_computation | convolution fusion | flops 805306368 | bytes 5242880 | tf_op jit(solution)/shard_map/cne,ep->cnp/dot_general | solution.py:559
Async XLA Ops:
  0.0 214.2 %copy-start = (bf16[512,1536]{1,0:T(8,128)(2,1)S(1)}, bf16[512,1536]{1,0:T(8,128)(2,1)}, u32[]{:S(2)}) copy-start(bf16[512,1536]{1,0:T(8,128)(2,1)} %param.33) | copy-start | bytes 4718596
